TPU v7x, 256 devices: a whole 4x4x8 slice. The times are simulated.
256 devices in a mesh: row: 32 (over z_lo, y, core), col: 8 (over x, z_hi).
Axes of the slice: x: 4, y: 4, z: 8 (z_hi: 2, z_lo: 4; z = z_hi * 4 + z_lo), core: 2. Of those that a mesh axis runs over, the one named last changes fastest.
Arguments:
- spectral_field: float32 [2, 256, 256, 256], P(None, 'row', 'col'), may hold values from -4.5 to 4.5
Outputs:
- updated_field: float32 [2, 256, 256, 256], P(None, 'row', 'col')
- shell_spectrum: float32 [256], replicated
All inputs are finite; a program needn't handle non-finite values.
Results may differ from a plain program's by a relative error of at most 0.0031.
Values may be sent and summed in bfloat16 or wider, within the bound.
A program may use at most 64 MiB of HBM per device.

v0:
```python
import functools
import math

import jax
import jax.numpy as jnp
import numpy as np
from jax import lax
from jax.experimental import pallas as pl
from jax.experimental.pallas import tpu as pltpu
from jax.sharding import PartitionSpec as P

PHASE_RATE = 0.0002
COUPLING = 0.2
K = 256
N = 512
BF16 = jnp.bfloat16
F32 = jnp.float32


def mm(a, b):
    return lax.dot_general(a, b, (((1,), (0,)), ((), ())), preferred_element_type=F32)


def mmt(a, b):
    return lax.dot_general(a, b, (((1,), (1,)), ((), ())), preferred_element_type=F32)


def iota(shape, dim):
    return lax.broadcasted_iota(jnp.int32, shape, dim)


def one_hot(hit):
    return jnp.where(hit, 1.0, 0.0).astype(BF16)


def transform_kernel(
    field, fwd, inv, out,
    p1, p2, p3, aout, bin_, yb, bout, cin, dz, cub, cout, din, dout, ein, zb,
    s1, r1, s2, r2, s3, r3, s4, r4,
):
    row = lax.axis_index("row")
    xh = lax.axis_index("col")
    zl = row // 8
    yc = row % 8

    def remote(src, dst, send, recv, to_row, to_col):
        return pltpu.make_async_remote_copy(
            src_ref=src, dst_ref=dst, send_sem=send, recv_sem=recv,
            device_id={"row": to_row, "col": to_col}, device_id_type=pl.DeviceIdType.MESH,
        )

    barrier = pltpu.get_barrier_semaphore()

    @pl.loop(1, 32)
    def _(i):
        d = (zl * 8 + xh + i) % 32
        pl.semaphore_signal(
            barrier, inc=1, device_id={"row": (d // 8) * 8 + yc, "col": d % 8},
            device_id_type=pl.DeviceIdType.MESH,
        )

    @pl.loop(1, 8)
    def _(j):
        pl.semaphore_signal(
            barrier, inc=1, device_id={"row": zl * 8 + (yc + j) % 8, "col": xh},
            device_id_type=pl.DeviceIdType.MESH,
        )

    def copy1(k, i):
        zd = (zl + 4 - k) % 4
        xd = (xh + i) % 8
        return remote(aout.at[zd, xd], bin_.at[zl, xh], s1.at[k, i], r1.at[k, i], zd * 8 + yc, xd)

    def copy2(k, j):
        zs = (zl + k) % 4
        yd = (yc + j) % 8
        return remote(bout.at[yd, :, zs], cin.at[yc, :, zs], s2.at[k, j], r2.at[k, j], zl * 8 + yd, xh)

    def copy3(k, j):
        zs = (zl + k) % 4
        yd = (yc + j) % 8
        return remote(cout.at[yd, zs], din.at[yc, zs], s3.at[k, j], r3.at[k, j], zl * 8 + yd, xh)

    def copy4(k, i):
        zd = (zl + k) % 4
        xd = (xh + i) % 8
        return remote(dout.at[zd, xd], ein.at[zl, xh], s4.at[k, i], r4.at[k, i], zd * 8 + yc, xd)

    def stage_a(k):
        zd = (zl + 4 - k) % 4
        rows = pl.ds(pl.multiple_of(zd * 128, 128), 128)
        c, s = inv[rows, :256], inv[rows, 256:]
        re = field[0].reshape(256, 256).astype(BF16)
        im = field[1].reshape(256, 256).astype(BF16)
        out_re = (mmt(c, re) - mmt(s, im)) * (1.0 / 16.0)
        out_im = (mmt(s, re) + mmt(c, im)) * (1.0 / 16.0)
        aout[zd, :, 0] = out_re.astype(BF16).reshape(8, 16, 256)
        aout[zd, :, 1] = out_im.astype(BF16).reshape(8, 16, 256)

    @pl.loop(0, 4)
    def _(k):
        stage_a(k)

    bin_[zl, xh] = aout[zl, xh]
    pl.semaphore_wait(barrier, 38)

    @pl.loop(1, 8)
    def _(i):
        copy1(0, i).start()

    @pl.loop(1, 4)
    def _(k):
        @pl.loop(0, 8)
        def _(i):
            copy1(k, i).start()

    j1 = iota((128, 512), 1)
    f1 = ((j1 // 32) % 4) * 128 + (j1 // 128) * 32 + j1 % 32

    @pl.loop(0, 4)
    def _(b):
        rows = pl.ds(pl.multiple_of(b * 128, 128), 128)
        p1[rows, :] = one_hot(iota((128, 512), 0) + b * 128 == f1)

    q2 = iota((256, 256), 0)
    p2[...] = one_hot(iota((256, 256), 1) == (q2 % 32) * 8 + q2 // 32)

    j3 = iota((128, 1024), 1)
    f3 = ((j3 // 16) % 8) * 128 + (j3 % 16) * 8 + j3 // 128

    @pl.loop(0, 8)
    def _(b):
        rows = pl.ds(pl.multiple_of(b * 128, 128), 128)
        p3[rows, :] = one_hot(iota((128, 1024), 0) + b * 128 == f3)

    def stage_b(k):
        zs = (zl + k) % 4
        parts = []
        for ht in range(2):
            for xt in range(2):
                lanes = slice(xt * 128, xt * 128 + 128)
                parts.append(jnp.concatenate(
                    [bin_[zs, ht * 4 + h, :, :, lanes].reshape(32, 128) for h in range(4)], axis=1))
        o = mm(jnp.concatenate(parts, axis=0), p1[...]).astype(BF16)
        for ht in range(2):
            for xt in range(2):
                base = (ht * 2 + xt) * 32
                for c in range(2):
                    for x in range(4):
                        yb[c, xt * 4 + x, :, ht * 128:ht * 128 + 128] = (
                            o[base + c * 16:base + c * 16 + 16, x * 128:x * 128 + 128])
        re = yb[0].reshape(128, 256)
        im = yb[1].reshape(128, 256)
        cos, sin = fwd[:256, :], fwd[256:, :]
        for c in range(2):
            if c == 0:
                v = (mm(re, cos) - mm(im, sin)) * (1.0 / 16.0)
            else:
                v = (mm(re, sin) + mm(im, cos)) * (1.0 / 16.0)
            for y in range(4):
                w = v[:, y * 128:y * 128 + 128].reshape(8, 2, 8, 128)
                for zh in range(2):
                    bout[y * 2 + zh, c, zs] = w[:, zh].astype(BF16)

    @pl.loop(0, 4)
    def _(k):
        @pl.when(k > 0)
        def _():
            copy1(k, 0).wait_recv()

        @pl.loop(1, 8)
        def _(i):
            copy1(k, i).wait_recv()

        stage_b(k)

        @pl.loop(1, 8)
        def _(j):
            copy2(k, j).start()

    cin[yc] = bout[yc]

    @pl.loop(0, 4)
    def _(k):
        @pl.loop(1, 8)
        def _(j):
            copy2(k, j).wait_recv()

    @pl.loop(0, 8)
    def _(s):
        d = jnp.concatenate([cin[s, 0].reshape(256, 128), cin[s, 1].reshape(256, 128)], axis=1)
        dz[:, :, s] = mm(p2[...], d).reshape(8, 4, 8, 256).astype(BF16)

    @pl.loop(0, 8)
    def _(z):
        d = dz[z].reshape(256, 256)
        d2 = jnp.concatenate([-d[:, 128:], d[:, :128]], axis=1)
        for h in range(4):
            rows = slice(h * 128, h * 128 + 128)
            phys = (mm(inv[rows, :256], d) + mm(inv[rows, 256:], d2)) * (1.0 / 16.0)
            re, im = phys[:, :128], phys[:, 128:]
            gain = COUPLING * (re * re + im * im)
            cub[rows, :128] = (gain * re).astype(BF16)
            cub[rows, 128:] = (gain * im).astype(BF16)
        m1 = mm(fwd[:256, :], cub[...])
        m2 = mm(fwd[256:, :], cub[...])
        back = ((m1[:, :128] + m2[:, 128:]) * (1.0 / 32.0), (m1[:, 128:] - m2[:, :128]) * (1.0 / 32.0))
        for c in range(2):
            v = back[c].reshape(4, 8, 8, 128)
            for q in range(4):
                cout[:, q, z, c] = v[q].astype(BF16)

    @pl.loop(0, 4)
    def _(k):
        @pl.loop(1, 8)
        def _(j):
            copy3(k, j).start()

    din[yc] = cout[yc]

    def stage_d(k):
        zs = (zl + k) % 4
        r = []
        for c in range(2):
            r.append(jnp.concatenate([
                jnp.concatenate([din[y * 2 + zh, zs, :, c].reshape(64, 128) for zh in range(2)], axis=0)
                for y in range(4)], axis=1))
        r = jnp.concatenate(r, axis=0)
        o1 = mmt(fwd[:256, :], r)
        o2 = mmt(fwd[256:, :], r)
        re = (o1[:, :128] + o2[:, 128:]) * (1.0 / 32.0)
        im = (o1[:, 128:] - o2[:, :128]) * (1.0 / 32.0)
        dout[zs, :, 0] = re.astype(BF16).reshape(8, 32, 128)
        dout[zs, :, 1] = im.astype(BF16).reshape(8, 32, 128)

    @pl.loop(0, 4)
    def _(k):
        @pl.loop(1, 8)
        def _(j):
            copy3(k, j).wait_recv()

        stage_d(k)

        @pl.when(k > 0)
        def _():
            copy4(k, 0).start()

        @pl.loop(1, 8)
        def _(i):
            copy4(k, i).start()

    ein[zl, xh] = dout[zl, xh]

    @pl.loop(0, 4)
    def _(k):
        @pl.when(k > 0)
        def _():
            copy4(k, 0).wait_recv()

        @pl.loop(1, 8)
        def _(i):
            copy4(k, i).wait_recv()

    for g in range(4):
        o = mm(jnp.concatenate([ein[g, s].reshape(64, 128) for s in range(8)], axis=1), p3[...]).astype(BF16)
        for c in range(2):
            for x in range(8):
                zb[c, x, :, g * 128:g * 128 + 128] = o[c * 32:c * 32 + 32, x * 128:x * 128 + 128]
    re = zb[0].reshape(256, 512)
    im = zb[1].reshape(256, 512)
    cos, sin = inv[:, :256], inv[:, 256:]
    out[0] = (mm(re, cos) + mm(im, sin)) * (1.0 / 32.0)
    out[1] = (mm(im, cos) - mm(re, sin)) * (1.0 / 32.0)

    @pl.loop(0, 4)
    def _(k):
        @pl.when(k > 0)
        def _():
            copy1(k, 0).wait_send()
            copy4(k, 0).wait_send()

        @pl.loop(1, 8)
        def _(i):
            copy1(k, i).wait_send()
            copy2(k, i).wait_send()
            copy3(k, i).wait_send()
            copy4(k, i).wait_send()


def update_kernel(field, nonlinear, updated, shells):
    wx0 = lax.axis_index("row") * 8 - 128
    wy0 = lax.axis_index("col") * 32 - 128
    wz = iota((1, 256), 1) - 128
    az = PHASE_RATE * (wz * wz).astype(F32)
    cz, sz = jnp.cos(az), jnp.sin(az)
    r = iota((256, 1), 0)
    wx = wx0 + r // 32
    wy = wy0 + r % 32
    r2 = wx * wx + wy * wy
    ar = PHASE_RATE * r2.astype(F32)
    cr, sr = jnp.cos(ar), jnp.sin(ar)
    cos = cr * cz - sr * sz
    sin = sr * cz + cr * sz
    u = field[0] - nonlinear[1]
    v = field[1] + nonlinear[0]
    re = u * cos + v * sin
    im = v * cos - u * sin
    updated[0] = re
    updated[1] = im
    energy = re * re + im * im
    j = jnp.abs(iota((256, 128), 0) - 128)
    within = jnp.where(j <= iota((256, 128), 1), 1.0, 0.0)
    prefix = lax.dot_general(energy, within, (((1,), (0,)), ((), ())),
                             preferred_element_type=F32, precision=lax.Precision.HIGHEST)
    parts = []
    for t in range(2):
        s = iota((1, 128), 1) + t * 128
        room = s * s + s - r2
        m = jnp.sqrt(jnp.maximum(room, 0).astype(F32) + 0.5).astype(jnp.int32)
        inner = jnp.take_along_axis(prefix, jnp.minimum(m, 127), axis=1, mode="promise_in_bounds")
        total = jnp.where(room >= 0, inner, 0.0) + jnp.where(room >= 128 * 128, energy[:, :1], 0.0)
        parts.append(jnp.sum(total, axis=0, keepdims=True))
    full = jnp.concatenate(parts, axis=1)
    lane = iota((1, 256), 1)
    shifted = jnp.concatenate([pltpu.roll(parts[0], 1, 1), pltpu.roll(parts[1], 1, 1)], axis=1)
    shifted = jnp.where(lane == 0, 0.0, jnp.where(lane == 128, parts[0][:, 127:], shifted))
    shells[...] = full - shifted


def reduce_kernel(shells, counts, out, first, second, mid, s1, r1, s2, r2):
    row = lax.axis_index("row")
    xh = lax.axis_index("col")
    zl = row // 8
    yc = row % 8
    me = zl * 8 + xh

    def copy1(i):
        d = (me + i) % 32
        return pltpu.make_async_remote_copy(
            src_ref=shells, dst_ref=first.at[me], send_sem=s1.at[i], recv_sem=r1.at[i],
            device_id={"row": (d // 8) * 8 + yc, "col": d % 8}, device_id_type=pl.DeviceIdType.MESH)

    def copy2(j):
        return pltpu.make_async_remote_copy(
            src_ref=mid, dst_ref=second.at[yc], send_sem=s2.at[j], recv_sem=r2.at[j],
            device_id={"row": zl * 8 + (yc + j) % 8, "col": xh}, device_id_type=pl.DeviceIdType.MESH)

    barrier = pltpu.get_barrier_semaphore()

    @pl.loop(1, 32)
    def _(i):
        d = (me + i) % 32
        pl.semaphore_signal(
            barrier, inc=1, device_id={"row": (d // 8) * 8 + yc, "col": d % 8},
            device_id_type=pl.DeviceIdType.MESH)

    @pl.loop(1, 8)
    def _(j):
        pl.semaphore_signal(
            barrier, inc=1, device_id={"row": zl * 8 + (yc + j) % 8, "col": xh},
            device_id_type=pl.DeviceIdType.MESH)

    first[me] = shells[...]
    pl.semaphore_wait(barrier, 38)

    @pl.loop(1, 32)
    def _(i):
        copy1(i).start()

    @pl.loop(1, 32)
    def _(i):
        copy1(i).wait_recv()

    mid[...] = jnp.sum(first[...], axis=0)
    second[yc] = mid[...]

    @pl.loop(1, 8)
    def _(j):
        copy2(j).start()

    @pl.loop(1, 8)
    def _(j):
        copy2(j).wait_recv()

    out[...] = jnp.sum(second[...], axis=0) / counts[...]

    @pl.loop(1, 32)
    def _(i):
        copy1(i).wait_send()

    @pl.loop(1, 8)
    def _(j):
        copy2(j).wait_send()


def tables():
    waves = np.arange(K, dtype=np.int64) - K // 2
    phase = (waves[:, None] * np.arange(N, dtype=np.int64)[None, :]) % N
    angle = phase.astype(np.float32) * np.float32(2.0 * math.pi / N)
    cos = np.cos(angle).astype(jnp.bfloat16)
    sin = np.sin(angle).astype(jnp.bfloat16)
    fwd = np.concatenate([cos, sin], axis=0)
    inv = np.concatenate([cos.T, sin.T], axis=1)
    sq = waves * waves
    q = (sq[:, None] + sq[None, :]).reshape(-1)
    pairs = np.bincount(q, minlength=2 * (K // 2) ** 2 + 1)
    counts = np.zeros(K, np.float64)
    radii = np.nonzero(pairs)[0]
    for w2 in sq:
        shell = np.floor(np.sqrt((radii + w2).astype(np.float64)) + 0.5).astype(np.int64)
        counts += np.bincount(shell, weights=pairs[radii], minlength=K)[:K]
    return fwd, np.ascontiguousarray(inv), np.maximum(counts, 1.0).astype(np.float32).reshape(1, K)


VMEM = pl.BlockSpec(memory_space=pltpu.VMEM)


def body(spectral_field, fwd, inv, counts):
    nonlinear = pl.pallas_call(
        transform_kernel,
        out_shape=jax.ShapeDtypeStruct((2, 256, 256), F32),
        in_specs=[VMEM] * 3,
        out_specs=VMEM,
        scratch_shapes=[
            pltpu.VMEM((512, 512), BF16),
            pltpu.VMEM((256, 256), BF16),
            pltpu.VMEM((1024, 1024), BF16),
            pltpu.VMEM((4, 8, 2, 16, 256), BF16),
            pltpu.VMEM((4, 8, 2, 16, 256), BF16),
            pltpu.VMEM((2, 8, 16, 256), BF16),
            pltpu.VMEM((8, 2, 4, 8, 8, 128), BF16),
            pltpu.VMEM((8, 2, 4, 8, 8, 128), BF16),
            pltpu.VMEM((8, 4, 8, 8, 256), BF16),
            pltpu.VMEM((512, 256), BF16),
            pltpu.VMEM((8, 4, 8, 2, 8, 128), BF16),
            pltpu.VMEM((8, 4, 8, 2, 8, 128), BF16),
            pltpu.VMEM((4, 8, 2, 32, 128), BF16),
            pltpu.VMEM((4, 8, 2, 32, 128), BF16),
            pltpu.VMEM((2, 8, 32, 512), BF16),
        ] + [pltpu.SemaphoreType.DMA((4, 8))] * 8,
        compiler_params=pltpu.CompilerParams(
            collective_id=0, has_side_effects=True, vmem_limit_bytes=48 * 1024 * 1024),
        name="transforms",
    )(spectral_field, fwd, inv)

    updated, shells = pl.pallas_call(
        update_kernel,
        out_shape=(jax.ShapeDtypeStruct((2, 256, 256), F32), jax.ShapeDtypeStruct((1, 256), F32)),
        in_specs=[VMEM] * 2,
        out_specs=(VMEM, VMEM),
        name="update",
    )(spectral_field.reshape(2, 256, 256), nonlinear)

    spectrum = pl.pallas_call(
        reduce_kernel,
        out_shape=jax.ShapeDtypeStruct((1, 256), F32),
        in_specs=[VMEM] * 2,
        out_specs=VMEM,
        scratch_shapes=[
            pltpu.VMEM((32, 1, 256), F32),
            pltpu.VMEM((8, 1, 256), F32),
            pltpu.VMEM((1, 256), F32),
            pltpu.SemaphoreType.DMA((32,)),
            pltpu.SemaphoreType.DMA((32,)),
            pltpu.SemaphoreType.DMA((8,)),
            pltpu.SemaphoreType.DMA((8,)),
        ],
        compiler_params=pltpu.CompilerParams(collective_id=1, has_side_effects=True),
        name="reduce",
    )(shells, counts)
    return updated.reshape(2, 8, 32, 256), spectrum.reshape(256)


def solution(mesh):
    fwd, inv, counts = tables()
    step = functools.partial(jax.shard_map, mesh=mesh, check_vma=False)

    def run(spectral_field):
        return step(
            lambda f: body(f, jnp.asarray(fwd), jnp.asarray(inv), jnp.asarray(counts)),
            in_specs=(P(None, "row", "col", None),),
            out_specs=(P(None, "row", "col", None), P()),
        )(spectral_field)

    return run
```

profile of v0, /device:TPU:1, one launch (start us, length us, event | category | flops | bytes accessed | tf_op | source)
XLA Modules:
  0.0 92.2 jit_solution(16547771219168734120)
XLA Ops:
  0.6 0.0 copy-start
  0.6 1.0 %copy-done = f32[2,8,32,256]{3,2,1,0:T(8,128)S(1)} copy-done((f32[2,8,32,256]{3,2,1,0:T(8,128)S(1)}, f32[2,8,32,256]{3,2,1,0:T(8,128)}, u32[]{:S(2)}) %copy-start) | copy-done | bytes 524312
  1.7 0.0 copy-start.2
  1.7 1.0 %copy-done.2 = bf16[512,512]{1,0:T(8,128)(2,1)S(1)} copy-done((bf16[512,512]{1,0:T(8,128)(2,1)S(1)}, bf16[512,512]{1,0:T(8,128)(2,1)}, u32[]{:S(2)}) %copy-start.2) | copy-done | bytes 524312
  2.7 0.0 copy-start.3
  2.7 1.0 %copy-done.3 = bf16[512,512]{1,0:T(8,128)(2,1)S(1)} copy-done((bf16[512,512]{1,0:T(8,128)(2,1)S(1)}, bf16[512,512]{1,0:T(8,128)(2,1)}, u32[]{:S(2)}) %copy-start.3) | copy-done | bytes 524312
  3.8 66.5 %transforms.1.nonlinear = f32[2,256,256]{2,1,0:T(8,128)S(1)} custom-call(f32[2,8,32,256]{3,2,1,0:T(8,128)S(1)} %copy-done, bf16[512,512]{1,0:T(8,128)(2,1)S(1)} %copy-done.3, bf16[512,512]{1,0:T(8,128)(2,1)S(1)} %copy-done.2), custom_call_target="tpu_custom_call" | custom-call | tf_op jit(solution)/shard_map/transforms/pallas_call | solution.py:419
  70.2 0.0 copy-start.1
  70.2 0.8 copy-done.1
  71.0 3.1 %update.1 = (f32[2,256,256]{2,1,0:T(8,128)}, f32[1,256]{1,0:T(1,128)}) custom-call(f32[2,256,256]{2,1,0:T(8,128)} %bitcast.3, f32[2,256,256]{2,1,0:T(8,128)} %copy-done.1), custom_call_target="tpu_custom_call" | custom-call | tf_op jit(solution)/shard_map/update/pallas_call | solution.py:446
  74.1 16.8 %reduce.1 = f32[1,256]{1,0:T(1,128)} custom-call(f32[1,256]{1,0:T(1,128)} %get-tuple-element.5.shells, f32[1,256]{1,0:T(1,128)} %constant.8.clone.counts), custom_call_target="tpu_custom_call" | custom-call | tf_op jit(solution)/shard_map/reduce/pallas_call | solution.py:454
  91.0 0.0 copy-start.4
  91.0 0.7 copy-done.4
  91.6 0.6 copy.7
Async XLA Ops:
  0.6 1.0 %copy-start = (f32[2,8,32,256]{3,2,1,0:T(8,128)S(1)}, f32[2,8,32,256]{3,2,1,0:T(8,128)}, u32[]{:S(2)}) copy-start(f32[2,8,32,256]{3,2,1,0:T(8,128)} %field.1) | copy-start | bytes 1572868
  1.7 1.0 %copy-start.2 = (bf16[512,512]{1,0:T(8,128)(2,1)S(1)}, bf16[512,512]{1,0:T(8,128)(2,1)}, u32[]{:S(2)}) copy-start(bf16[512,512]{1,0:T(8,128)(2,1)} %constant.7.clone.inv) | copy-start | bytes 1572868
  2.7 1.0 %copy-start.3 = (bf16[512,512]{1,0:T(8,128)(2,1)S(1)}, bf16[512,512]{1,0:T(8,128)(2,1)}, u32[]{:S(2)}) copy-start(bf16[512,512]{1,0:T(8,128)(2,1)} %constant.6.clone.fwd) | copy-start | bytes 1572868
  70.2 0.8 copy-start.1
  91.0 0.7 copy-start.4
where the time goes:
time: 92.5 us; the launch traced here: 92.2 us
  Pallas kernels  86.4 us (93%)
  local copies, waits for them, and re-layouts  5.12 us (6%)
    pallas_call x1, Pallas kernels, body(): pl.pallas_call(transform_kernel, out_shape=jax.ShapeDtypeStruct((2, 256,...  66.5 us
    pallas_call x1, Pallas kernels, body(): pl.pallas_call(reduce_kernel, out_shape=jax.ShapeDtypeStruct((1, 256), F3...  16.8 us
    unnamed x11, local copies, waits for them, and re-layouts  5.12 us
    pallas_call x1, Pallas kernels, body(): pl.pallas_call(update_kernel, out_shape=(jax.ShapeDtypeStruct((2, 256, 25...  3.1 us

commit v1 on v0

--- a/solution.py
+++ b/solution.py
@@ -33,10 +33,30 @@
     return jnp.where(hit, 1.0, 0.0).astype(BF16)
 
 
+def shell_sums(energy, r2):
+    j = jnp.abs(iota((256, 128), 0) - 128)
+    within = jnp.where(j <= iota((256, 128), 1), 1.0, 0.0)
+    prefix = lax.dot_general(energy, within, (((1,), (0,)), ((), ())),
+                             preferred_element_type=F32, precision=lax.Precision.HIGHEST)
+    parts = []
+    for t in range(2):
+        s = iota((1, 128), 1) + t * 128
+        room = s * s + s - r2
+        m = jnp.sqrt(jnp.maximum(room, 0).astype(F32) + 0.5).astype(jnp.int32)
+        inner = jnp.take_along_axis(prefix, jnp.minimum(m, 127), axis=1, mode="promise_in_bounds")
+        total = jnp.where(room >= 0, inner, 0.0) + jnp.where(room >= 128 * 128, energy[:, :1], 0.0)
+        parts.append(jnp.sum(total, axis=0, keepdims=True))
+    lane = iota((1, 256), 1)
+    shifted = jnp.concatenate([pltpu.roll(parts[0], 1, 1), pltpu.roll(parts[1], 1, 1)], axis=1)
+    shifted = jnp.where(lane == 0, 0.0, jnp.where(lane == 128, parts[0][:, 127:], shifted))
+    return jnp.concatenate(parts, axis=1) - shifted
+
+
 def transform_kernel(
-    field, fwd, inv, out,
-    p1, p2, p3, aout, bin_, yb, bout, cin, dz, cub, cout, din, dout, ein, zb,
-    s1, r1, s2, r2, s3, r3, s4, r4,
+    field_hbm, fwd_hbm, inv_hbm, counts, out, spectrum,
+    field, fwd, inv, p1, p2, p3, aout, bin_, yb, bout, cin, dz, cub, cout, din, dout, ein, zb,
+    shells, first, second, mid,
+    s1, r1, s2, r2, s3, r3, s4, r4, load_sem, s5, r5, s6, r6,
 ):
     row = lax.axis_index("row")
     xh = lax.axis_index("col")
@@ -48,6 +68,14 @@
             src_ref=src, dst_ref=dst, send_sem=send, recv_sem=recv,
             device_id={"row": to_row, "col": to_col}, device_id_type=pl.DeviceIdType.MESH,
         )
+
+    loads = [
+        pltpu.make_async_copy(field_hbm, field, load_sem.at[0]),
+        pltpu.make_async_copy(inv_hbm, inv, load_sem.at[1]),
+        pltpu.make_async_copy(fwd_hbm, fwd, load_sem.at[2]),
+    ]
+    for load in loads:
+        load.start()
 
     barrier = pltpu.get_barrier_semaphore()
 
@@ -85,6 +113,34 @@
         zd = (zl + k) % 4
         xd = (xh + i) % 8
         return remote(dout.at[zd, xd], ein.at[zl, xh], s4.at[k, i], r4.at[k, i], zd * 8 + yc, xd)
+
+    me1 = zl * 8 + xh
+
+    def copy5(i):
+        d = (me1 + i) % 32
+        return remote(shells, first.at[me1], s5.at[i], r5.at[i], (d // 8) * 8 + yc, d % 8)
+
+    def copy6(j):
+        return remote(mid, second.at[yc], s6.at[j], r6.at[j], zl * 8 + (yc + j) % 8, xh)
+
+    j1 = iota((128, 512), 1)
+    f1 = ((j1 // 32) % 4) * 128 + (j1 // 128) * 32 + j1 % 32
+
+    @pl.loop(0, 4)
+    def _(b):
+        rows = pl.ds(pl.multiple_of(b * 128, 128), 128)
+        p1[rows, :] = one_hot(iota((128, 512), 0) + b * 128 == f1)
+
+    q2 = iota((256, 256), 0)
+    p2[...] = one_hot(iota((256, 256), 1) == (q2 % 32) * 8 + q2 // 32)
+
+    j3 = iota((128, 1024), 1)
+    f3 = ((j3 // 16) % 8) * 128 + (j3 % 16) * 8 + j3 // 128
+
+    @pl.loop(0, 8)
+    def _(b):
+        rows = pl.ds(pl.multiple_of(b * 128, 128), 128)
+        p3[rows, :] = one_hot(iota((128, 1024), 0) + b * 128 == f3)
 
     def stage_a(k):
         zd = (zl + 4 - k) % 4
@@ -97,6 +153,9 @@
         aout[zd, :, 0] = out_re.astype(BF16).reshape(8, 16, 256)
         aout[zd, :, 1] = out_im.astype(BF16).reshape(8, 16, 256)
 
+    loads[0].wait()
+    loads[1].wait()
+
     @pl.loop(0, 4)
     def _(k):
         stage_a(k)
@@ -113,25 +172,6 @@
         @pl.loop(0, 8)
         def _(i):
             copy1(k, i).start()
-
-    j1 = iota((128, 512), 1)
-    f1 = ((j1 // 32) % 4) * 128 + (j1 // 128) * 32 + j1 % 32
-
-    @pl.loop(0, 4)
-    def _(b):
-        rows = pl.ds(pl.multiple_of(b * 128, 128), 128)
-        p1[rows, :] = one_hot(iota((128, 512), 0) + b * 128 == f1)
-
-    q2 = iota((256, 256), 0)
-    p2[...] = one_hot(iota((256, 256), 1) == (q2 % 32) * 8 + q2 // 32)
-
-    j3 = iota((128, 1024), 1)
-    f3 = ((j3 // 16) % 8) * 128 + (j3 % 16) * 8 + j3 // 128
-
-    @pl.loop(0, 8)
-    def _(b):
-        rows = pl.ds(pl.multiple_of(b * 128, 128), 128)
-        p3[rows, :] = one_hot(iota((128, 1024), 0) + b * 128 == f3)
 
     def stage_b(k):
         zs = (zl + k) % 4
@@ -162,6 +202,8 @@
                 for zh in range(2):
                     bout[y * 2 + zh, c, zs] = w[:, zh].astype(BF16)
 
+    loads[2].wait()
+
     @pl.loop(0, 4)
     def _(k):
         @pl.when(k > 0)
@@ -269,8 +311,51 @@
     re = zb[0].reshape(256, 512)
     im = zb[1].reshape(256, 512)
     cos, sin = inv[:, :256], inv[:, 256:]
-    out[0] = (mm(re, cos) + mm(im, sin)) * (1.0 / 32.0)
-    out[1] = (mm(im, cos) - mm(re, sin)) * (1.0 / 32.0)
+    nl_re = (mm(re, cos) + mm(im, sin)) * (1.0 / 32.0)
+    nl_im = (mm(im, cos) - mm(re, sin)) * (1.0 / 32.0)
+    u = field[0].reshape(256, 256) - nl_im
+    v = field[1].reshape(256, 256) + nl_re
+    out[0] = u.reshape(8, 32, 256)
+    out[1] = v.reshape(8, 32, 256)
+
+    wz = iota((1, 256), 1) - 128
+    r = iota((256, 1), 0)
+    wx = row * 8 - 128 + r // 32
+    wy = xh * 32 - 128 + r % 32
+    rad2 = wx * wx + wy * wy
+    shells[...] = shell_sums(u * u + v * v, rad2)
+    first[me1] = shells[...]
+
+    @pl.loop(1, 32)
+    def _(i):
+        copy5(i).start()
+
+    az = PHASE_RATE * (wz * wz).astype(F32)
+    ar = PHASE_RATE * rad2.astype(F32)
+    cz, sz = jnp.cos(az), jnp.sin(az)
+    cr, sr = jnp.cos(ar), jnp.sin(ar)
+    cos = (cr * cz - sr * sz).reshape(8, 32, 256)
+    sin = (sr * cz + cr * sz).reshape(8, 32, 256)
+    u, v = out[0], out[1]
+    out[0] = u * cos + v * sin
+    out[1] = v * cos - u * sin
+
+    @pl.loop(1, 32)
+    def _(i):
+        copy5(i).wait_recv()
+
+    mid[...] = jnp.sum(first[...], axis=0)
+    second[yc] = mid[...]
+
+    @pl.loop(1, 8)
+    def _(j):
+        copy6(j).start()
+
+    @pl.loop(1, 8)
+    def _(j):
+        copy6(j).wait_recv()
+
+    spectrum[...] = jnp.sum(second[...], axis=0) / counts[...]
 
     @pl.loop(0, 4)
     def _(k):
@@ -286,111 +371,13 @@
             copy3(k, i).wait_send()
             copy4(k, i).wait_send()
 
-
-def update_kernel(field, nonlinear, updated, shells):
-    wx0 = lax.axis_index("row") * 8 - 128
-    wy0 = lax.axis_index("col") * 32 - 128
-    wz = iota((1, 256), 1) - 128
-    az = PHASE_RATE * (wz * wz).astype(F32)
-    cz, sz = jnp.cos(az), jnp.sin(az)
-    r = iota((256, 1), 0)
-    wx = wx0 + r // 32
-    wy = wy0 + r % 32
-    r2 = wx * wx + wy * wy
-    ar = PHASE_RATE * r2.astype(F32)
-    cr, sr = jnp.cos(ar), jnp.sin(ar)
-    cos = cr * cz - sr * sz
-    sin = sr * cz + cr * sz
-    u = field[0] - nonlinear[1]
-    v = field[1] + nonlinear[0]
-    re = u * cos + v * sin
-    im = v * cos - u * sin
-    updated[0] = re
-    updated[1] = im
-    energy = re * re + im * im
-    j = jnp.abs(iota((256, 128), 0) - 128)
-    within = jnp.where(j <= iota((256, 128), 1), 1.0, 0.0)
-    prefix = lax.dot_general(energy, within, (((1,), (0,)), ((), ())),
-                             preferred_element_type=F32, precision=lax.Precision.HIGHEST)
-    parts = []
-    for t in range(2):
-        s = iota((1, 128), 1) + t * 128
-        room = s * s + s - r2
-        m = jnp.sqrt(jnp.maximum(room, 0).astype(F32) + 0.5).astype(jnp.int32)
-        inner = jnp.take_along_axis(prefix, jnp.minimum(m, 127), axis=1, mode="promise_in_bounds")
-        total = jnp.where(room >= 0, inner, 0.0) + jnp.where(room >= 128 * 128, energy[:, :1], 0.0)
-        parts.append(jnp.sum(total, axis=0, keepdims=True))
-    full = jnp.concatenate(parts, axis=1)
-    lane = iota((1, 256), 1)
-    shifted = jnp.concatenate([pltpu.roll(parts[0], 1, 1), pltpu.roll(parts[1], 1, 1)], axis=1)
-    shifted = jnp.where(lane == 0, 0.0, jnp.where(lane == 128, parts[0][:, 127:], shifted))
-    shells[...] = full - shifted
-
-
-def reduce_kernel(shells, counts, out, first, second, mid, s1, r1, s2, r2):
-    row = lax.axis_index("row")
-    xh = lax.axis_index("col")
-    zl = row // 8
-    yc = row % 8
-    me = zl * 8 + xh
-
-    def copy1(i):
-        d = (me + i) % 32
-        return pltpu.make_async_remote_copy(
-            src_ref=shells, dst_ref=first.at[me], send_sem=s1.at[i], recv_sem=r1.at[i],
-            device_id={"row": (d // 8) * 8 + yc, "col": d % 8}, device_id_type=pl.DeviceIdType.MESH)
-
-    def copy2(j):
-        return pltpu.make_async_remote_copy(
-            src_ref=mid, dst_ref=second.at[yc], send_sem=s2.at[j], recv_sem=r2.at[j],
-            device_id={"row": zl * 8 + (yc + j) % 8, "col": xh}, device_id_type=pl.DeviceIdType.MESH)
-
-    barrier = pltpu.get_barrier_semaphore()
-
     @pl.loop(1, 32)
     def _(i):
-        d = (me + i) % 32
-        pl.semaphore_signal(
-            barrier, inc=1, device_id={"row": (d // 8) * 8 + yc, "col": d % 8},
-            device_id_type=pl.DeviceIdType.MESH)
+        copy5(i).wait_send()
 
     @pl.loop(1, 8)
     def _(j):
-        pl.semaphore_signal(
-            barrier, inc=1, device_id={"row": zl * 8 + (yc + j) % 8, "col": xh},
-            device_id_type=pl.DeviceIdType.MESH)
-
-    first[me] = shells[...]
-    pl.semaphore_wait(barrier, 38)
-
-    @pl.loop(1, 32)
-    def _(i):
-        copy1(i).start()
-
-    @pl.loop(1, 32)
-    def _(i):
-        copy1(i).wait_recv()
-
-    mid[...] = jnp.sum(first[...], axis=0)
-    second[yc] = mid[...]
-
-    @pl.loop(1, 8)
-    def _(j):
-        copy2(j).start()
-
-    @pl.loop(1, 8)
-    def _(j):
-        copy2(j).wait_recv()
-
-    out[...] = jnp.sum(second[...], axis=0) / counts[...]
-
-    @pl.loop(1, 32)
-    def _(i):
-        copy1(i).wait_send()
-
-    @pl.loop(1, 8)
-    def _(j):
-        copy2(j).wait_send()
+        copy6(j).wait_send()
 
 
 def tables():
@@ -413,15 +400,22 @@
 
 
 VMEM = pl.BlockSpec(memory_space=pltpu.VMEM)
+HBM = pl.BlockSpec(memory_space=pltpu.HBM)
 
 
 def body(spectral_field, fwd, inv, counts):
-    nonlinear = pl.pallas_call(
+    updated, spectrum = pl.pallas_call(
         transform_kernel,
-        out_shape=jax.ShapeDtypeStruct((2, 256, 256), F32),
-        in_specs=[VMEM] * 3,
-        out_specs=VMEM,
+        out_shape=(
+            jax.ShapeDtypeStruct((2, 8, 32, 256), F32),
+            jax.ShapeDtypeStruct((1, 256), F32),
+        ),
+        in_specs=[HBM, HBM, HBM, VMEM],
+        out_specs=(VMEM, VMEM),
         scratch_shapes=[
+            pltpu.VMEM((2, 8, 32, 256), F32),
+            pltpu.VMEM((512, 512), BF16),
+            pltpu.VMEM((512, 512), BF16),
             pltpu.VMEM((512, 512), BF16),
             pltpu.VMEM((256, 256), BF16),
             pltpu.VMEM((1024, 1024), BF16),
@@ -437,38 +431,22 @@
             pltpu.VMEM((4, 8, 2, 32, 128), BF16),
             pltpu.VMEM((4, 8, 2, 32, 128), BF16),
             pltpu.VMEM((2, 8, 32, 512), BF16),
-        ] + [pltpu.SemaphoreType.DMA((4, 8))] * 8,
-        compiler_params=pltpu.CompilerParams(
-            collective_id=0, has_side_effects=True, vmem_limit_bytes=48 * 1024 * 1024),
-        name="transforms",
-    )(spectral_field, fwd, inv)
-
-    updated, shells = pl.pallas_call(
-        update_kernel,
-        out_shape=(jax.ShapeDtypeStruct((2, 256, 256), F32), jax.ShapeDtypeStruct((1, 256), F32)),
-        in_specs=[VMEM] * 2,
-        out_specs=(VMEM, VMEM),
-        name="update",
-    )(spectral_field.reshape(2, 256, 256), nonlinear)
-
-    spectrum = pl.pallas_call(
-        reduce_kernel,
-        out_shape=jax.ShapeDtypeStruct((1, 256), F32),
-        in_specs=[VMEM] * 2,
-        out_specs=VMEM,
-        scratch_shapes=[
+            pltpu.VMEM((1, 256), F32),
             pltpu.VMEM((32, 1, 256), F32),
             pltpu.VMEM((8, 1, 256), F32),
             pltpu.VMEM((1, 256), F32),
+        ] + [pltpu.SemaphoreType.DMA((4, 8))] * 8 + [
+            pltpu.SemaphoreType.DMA((3,)),
             pltpu.SemaphoreType.DMA((32,)),
             pltpu.SemaphoreType.DMA((32,)),
             pltpu.SemaphoreType.DMA((8,)),
             pltpu.SemaphoreType.DMA((8,)),
         ],
-        compiler_params=pltpu.CompilerParams(collective_id=1, has_side_effects=True),
-        name="reduce",
-    )(shells, counts)
-    return updated.reshape(2, 8, 32, 256), spectrum.reshape(256)
+        compiler_params=pltpu.CompilerParams(
+            collective_id=0, has_side_effects=True, vmem_limit_bytes=67000000),
+        name="transforms",
+    )(spectral_field, fwd, inv, counts)
+    return updated, spectrum.reshape(256)
 
 
 def solution(mesh):

time: 92.5 us -> 83.4 us (0.902)
  Pallas kernels: 86.4 us -> 80.2 us
  local copies, waits for them, and re-layouts: 5.12 us -> 2.45 us
    pallas_call x3 -> x1, Pallas kernels: 86.4 us -> 80.2 us  [body(): pl.pallas_call(transform_kernel, out_shape=(jax.ShapeDtypeStruct((2, 8, 3...]
    unnamed x11 -> x4, local copies, waits for them, and re-layouts: 5.12 us -> 2.45 us
where the time goes in v1:
time: 83.4 us; the launch traced here: 83.3 us
  Pallas kernels  80.2 us (96%)
  local copies, waits for them, and re-layouts  2.45 us (3%)
    pallas_call x1, Pallas kernels, body(): pl.pallas_call(transform_kernel, out_shape=(jax.ShapeDtypeStruct((2, 8, 3...  80.2 us
    unnamed x4, local copies, waits for them, and re-layouts  2.45 us

profile of v1, /device:TPU:1, one launch (start us, length us, event | category | flops | bytes accessed | tf_op | source)
XLA Modules:
  0.0 83.3 jit_solution(7025054084714114171)
XLA Ops:
  0.6 80.2 %transforms.1 = (f32[2,8,32,256]{3,2,1,0:T(8,128)}, f32[1,256]{1,0:T(1,128)}) custom-call(f32[2,8,32,256]{3,2,1,0:T(8,128)} %field_hbm.1, bf16[512,512]{1,0:T(8,128)(2,1)} %constant.6.clone.fwd_hbm, bf16[512,512]{1,0:T(8,128)(2,1)} %constant.7.clone.inv_hbm, f32[1,256]{1,0:T(1,128)} %constant.8.clone.counts), custom_call_target="tpu_custom_call" | custom-call | tf_op jit(solution)/shard_map/transforms/pallas_call | solution.py:407
  80.8 0.0 copy-start
  80.8 1.9 %copy.8 = f32[2,8,32,256]{3,2,1,0:T(8,128)} copy(f32[2,8,32,256]{3,2,1,0:T(8,128)} %get-tuple-element.8) | data formatting | bytes 1048576
  82.7 0.0 copy-done
  82.7 0.6 copy.9
Async XLA Ops:
  80.8 1.9 %copy-start = (f32[1,256]{1,0:T(1,128)S(1)}, f32[1,256]{1,0:T(1,128)}, u32[]{:S(2)}) copy-start(f32[1,256]{1,0:T(1,128)} %get-tuple-element.5) | copy-start | bytes 3076

commit v2 on v1

v2 whole, which is shorter than its diff:
```python
import functools
import math

import jax
import jax.numpy as jnp
import numpy as np
from jax import lax
from jax.experimental import pallas as pl
from jax.experimental.pallas import tpu as pltpu
from jax.sharding import PartitionSpec as P

PHASE_RATE = 0.0002
COUPLING = 0.2
K = 256
N = 512
BF16 = jnp.bfloat16
F32 = jnp.float32


def mm(a, b):
    return lax.dot_general(a, b, (((1,), (0,)), ((), ())), preferred_element_type=F32)


def mmt(a, b):
    return lax.dot_general(a, b, (((1,), (1,)), ((), ())), preferred_element_type=F32)


def iota(shape, dim):
    return lax.broadcasted_iota(jnp.int32, shape, dim)


def one_hot(hit):
    return jnp.where(hit, 1.0, 0.0).astype(BF16)


def shell_sums(energy, r2):
    j = jnp.abs(iota((256, 128), 0) - 128)
    within = jnp.where(j <= iota((256, 128), 1), 1.0, 0.0)
    prefix = lax.dot_general(energy, within, (((1,), (0,)), ((), ())),
                             preferred_element_type=F32, precision=lax.Precision.HIGHEST)
    parts = []
    for t in range(2):
        s = iota((1, 128), 1) + t * 128
        room = s * s + s - r2
        m = jnp.sqrt(jnp.maximum(room, 0).astype(F32) + 0.5).astype(jnp.int32)
        inner = jnp.take_along_axis(prefix, jnp.minimum(m, 127), axis=1, mode="promise_in_bounds")
        total = jnp.where(room >= 0, inner, 0.0) + jnp.where(room >= 128 * 128, energy[:, :1], 0.0)
        parts.append(jnp.sum(total, axis=0, keepdims=True))
    lane = iota((1, 256), 1)
    shifted = jnp.concatenate([pltpu.roll(parts[0], 1, 1), pltpu.roll(parts[1], 1, 1)], axis=1)
    shifted = jnp.where(lane == 0, 0.0, jnp.where(lane == 128, parts[0][:, 127:], shifted))
    return jnp.concatenate(parts, axis=1) - shifted


def transform_kernel(
    field_hbm, fwd_hbm, inv_hbm, last_hbm, counts, out, spectrum,
    field, fwd, inv, last, p1, p2, p3, aout, bin_, yb, bout, cin, cub, cout, din, dout, ein, zb,
    shells, first, second, mid,
    s1, r1, s2, r2, s3, r3, s4, r4, load_sem, s5, r5, s6, r6,
):
    row = lax.axis_index("row")
    xh = lax.axis_index("col")
    zl = row // 8
    yc = row % 8

    def remote(src, dst, send, recv, to_row, to_col):
        return pltpu.make_async_remote_copy(
            src_ref=src, dst_ref=dst, send_sem=send, recv_sem=recv,
            device_id={"row": to_row, "col": to_col}, device_id_type=pl.DeviceIdType.MESH,
        )

    loads = [
        pltpu.make_async_copy(field_hbm, field, load_sem.at[0]),
        pltpu.make_async_copy(inv_hbm, inv, load_sem.at[1]),
        pltpu.make_async_copy(fwd_hbm, fwd, load_sem.at[2]),
        pltpu.make_async_copy(last_hbm, last, load_sem.at[3]),
    ]
    for load in loads:
        load.start()

    barrier = pltpu.get_barrier_semaphore()

    @pl.loop(1, 32)
    def _(i):
        d = (zl * 8 + xh + i) % 32
        pl.semaphore_signal(
            barrier, inc=1, device_id={"row": (d // 8) * 8 + yc, "col": d % 8},
            device_id_type=pl.DeviceIdType.MESH,
        )

    @pl.loop(1, 8)
    def _(j):
        pl.semaphore_signal(
            barrier, inc=1, device_id={"row": zl * 8 + (yc + j) % 8, "col": xh},
            device_id_type=pl.DeviceIdType.MESH,
        )

    def copy1(h, k, i):
        zd = (zl + 4 - k) % 4
        xd = (xh + i) % 8
        return remote(aout.at[h, zd, xd], bin_.at[h, zl, xh], s1.at[h, k, i], r1.at[h, k, i], zd * 8 + yc, xd)

    def copy2(h, k, j):
        zs = (zl + k) % 4
        yd = (yc + j) % 8
        return remote(bout.at[h, yd, zs], cin.at[h, zs, yc], s2.at[h, k, j], r2.at[h, k, j], zl * 8 + yd, xh)

    def copy3(h, k, j):
        zs = (zl + k) % 4
        yd = (yc + j) % 8
        return remote(cout.at[h, yd, zs], din.at[h, yc, zs], s3.at[h, k, j], r3.at[h, k, j], zl * 8 + yd, xh)

    def copy4(h, k, i):
        zd = (zl + k) % 4
        xd = (xh + i) % 8
        return remote(dout.at[h, zd, xd], ein.at[h, zl, xh], s4.at[h, k, i], r4.at[h, k, i], zd * 8 + yc, xd)

    me1 = zl * 8 + xh

    def copy5(i):
        d = (me1 + i) % 32
        return remote(shells, first.at[me1], s5.at[i], r5.at[i], (d // 8) * 8 + yc, d % 8)

    def copy6(j):
        return remote(mid, second.at[yc], s6.at[j], r6.at[j], zl * 8 + (yc + j) % 8, xh)

    j1 = iota((128, 512), 1)
    f1 = ((j1 // 32) % 4) * 128 + (j1 // 128) * 32 + j1 % 32

    @pl.loop(0, 4)
    def _(b):
        rows = pl.ds(pl.multiple_of(b * 128, 128), 128)
        p1[rows, :] = one_hot(iota((128, 512), 0) + b * 128 == f1)

    q2 = iota((128, 128), 0)
    p2[...] = one_hot(iota((128, 128), 1) == (q2 // 64) * 64 + (q2 % 8) * 8 + (q2 // 8) % 8)

    j3 = iota((128, 1024), 1)
    f3 = ((j3 // 8) % 8) * 128 + ((j3 // 64) % 2) * 64 + (j3 % 8) * 8 + j3 // 128

    @pl.loop(0, 8)
    def _(b):
        rows = pl.ds(pl.multiple_of(b * 128, 128), 128)
        p3[rows, :] = one_hot(iota((128, 1024), 0) + b * 128 == f3)

    loads[0].wait()
    loads[1].wait()

    @pl.loop(0, 4)
    def _(zd):
        rows = pl.ds(pl.multiple_of(zd * 128, 128), 128)
        c, s = inv[rows, :256], inv[rows, 256:]
        re = field[0].reshape(256, 256).astype(BF16)
        im = field[1].reshape(256, 256).astype(BF16)
        pair = (
            (mmt(c, re) - mmt(s, im)) * (1.0 / 16.0),
            (mmt(s, re) + mmt(c, im)) * (1.0 / 16.0),
        )
        for ri in range(2):
            v = pair[ri].reshape(8, 2, 8, 256)
            for h in range(2):
                aout[h, zd, :, ri] = v[:, h].astype(BF16)

    for h in range(2):
        bin_[h, zl, xh] = aout[h, zl, xh]
    pl.semaphore_wait(barrier, 38)

    @pl.loop(0, 2)
    def _(h):
        @pl.loop(1, 8)
        def _(i):
            copy1(h, 0, i).start()

        @pl.loop(1, 4)
        def _(k):
            @pl.loop(0, 8)
            def _(i):
                copy1(h, k, i).start()

    loads[2].wait()
    loads[3].wait()

    def stage_b(h, k):
        zs = (zl + k) % 4
        parts = []
        for ht in range(2):
            for xt in range(2):
                lanes = slice(xt * 128, xt * 128 + 128)
                parts.append(jnp.concatenate(
                    [bin_[h, zs, ht * 4 + q, :, :, lanes].reshape(16, 128) for q in range(4)], axis=1))
        o = mm(jnp.concatenate(parts, axis=0), p1[...])
        for ht in range(2):
            for xt in range(2):
                base = (ht * 2 + xt) * 16
                for c in range(2):
                    for x in range(4):
                        yb[c, xt * 4 + x, :, ht * 128:ht * 128 + 128] = (
                            o[base + c * 8:base + c * 8 + 8, x * 128:x * 128 + 128].astype(BF16))
        q = mm(p2[...], yb[...].reshape(128, 256)).astype(BF16)
        mc = mm(q, fwd[:256, :])
        ms = mm(q, fwd[256:, :])
        pair = ((mc[:64] - ms[64:]) * (1.0 / 16.0), (ms[:64] + mc[64:]) * (1.0 / 16.0))
        for c in range(2):
            for y in range(4):
                w = pair[c][:, y * 128:y * 128 + 128].reshape(2, 4, 8, 128)
                for zh in range(2):
                    bout[h, y * 2 + zh, zs, :, c] = w[zh].astype(BF16)
        cin[h, zs, yc] = bout[h, yc, zs]

    @pl.loop(0, 2)
    def _(h):
        @pl.loop(0, 4)
        def _(k):
            @pl.when(k > 0)
            def _():
                copy1(h, k, 0).wait_recv()

            @pl.loop(1, 8)
            def _(i):
                copy1(h, k, i).wait_recv()

            stage_b(h, k)

            @pl.loop(1, 8)
            def _(j):
                copy2(h, k, j).start()

    def stage_c(h, z, slot):
        d = jnp.concatenate([cin[h, :, :, z, 0].reshape(256, 128), cin[h, :, :, z, 1].reshape(256, 128)], axis=1)
        d = jnp.concatenate([d, jnp.concatenate([-d[:, 128:], d[:, :128]], axis=1)], axis=0)
        for half in range(2):
            rows = slice(half * 256, half * 256 + 256)
            phys = mm(inv[rows, :], d) * (1.0 / 16.0)
            re, im = phys[:, :128], phys[:, 128:]
            gain = COUPLING * (re * re + im * im)
            cub[slot, rows, :128] = (gain * re).astype(BF16)
            cub[slot, rows, 128:] = (gain * im).astype(BF16)

    def stage_c_back(h, z, slot):
        m = mm(fwd[...], cub[slot])
        pair = (
            (m[:256, :128] + m[256:, 128:]) * (1.0 / 32.0),
            (m[:256, 128:] - m[256:, :128]) * (1.0 / 32.0),
        )
        for c in range(2):
            v = pair[c].reshape(4, 8, 8, 128)
            for q in range(4):
                cout[h, :, q, z, c] = v[q].astype(BF16)

    @pl.loop(0, 2)
    def _(h):
        @pl.loop(0, 4)
        def _(k):
            @pl.loop(1, 8)
            def _(j):
                copy2(h, k, j).wait_recv()

        @pl.loop(0, 2)
        def _(z):
            stage_c(h, 2 * z, 0)
            stage_c(h, 2 * z + 1, 1)
            stage_c_back(h, 2 * z, 0)
            stage_c_back(h, 2 * z + 1, 1)

        @pl.loop(0, 4)
        def _(k):
            @pl.loop(1, 8)
            def _(j):
                copy3(h, k, j).start()

        din[h, yc] = cout[h, yc]

    def stage_d(h, k):
        zs = (zl + k) % 4
        r = []
        for c in range(2):
            r.append(jnp.concatenate([
                jnp.concatenate([din[h, y * 2 + zh, zs, :, c].reshape(32, 128) for zh in range(2)], axis=0)
                for y in range(4)], axis=1))
        o = mmt(fwd[:256, :], jnp.concatenate(r, axis=0)) + mmt(fwd[256:, :], jnp.concatenate([r[1], -r[0]], axis=0))
        dout[h, zs] = (o * (1.0 / 32.0)).astype(BF16).reshape(8, 32, 128)

    @pl.loop(0, 2)
    def _(h):
        @pl.loop(0, 4)
        def _(k):
            @pl.loop(1, 8)
            def _(j):
                copy3(h, k, j).wait_recv()

            stage_d(h, k)

            @pl.when(k > 0)
            def _():
                copy4(h, k, 0).start()

            @pl.loop(1, 8)
            def _(i):
                copy4(h, k, i).start()

        ein[h, zl, xh] = dout[h, zl, xh]

    for h in range(2):
        @pl.loop(0, 4)
        def _(k, h=h):
            @pl.when(k > 0)
            def _():
                copy4(h, k, 0).wait_recv()

            @pl.loop(1, 8)
            def _(i):
                copy4(h, k, i).wait_recv()

        parts = [jnp.concatenate([ein[h, g, s] for s in range(8)], axis=1) for g in range(4)]
        o = mm(jnp.concatenate(parts, axis=0), p3[...]).astype(BF16)
        for g in range(4):
            for x in range(8):
                zb[x, :, (h * 4 + g) * 128:(h * 4 + g) * 128 + 128] = o[g * 32:g * 32 + 32, x * 128:x * 128 + 128]
    nl = mm(zb[...].reshape(256, 1024), last[...]) * (1.0 / 32.0)
    nl_re, nl_im = nl[:, :256], nl[:, 256:]
    u = field[0].reshape(256, 256) - nl_im
    v = field[1].reshape(256, 256) + nl_re
    out[0] = u.reshape(8, 32, 256)
    out[1] = v.reshape(8, 32, 256)

    wz = iota((1, 256), 1) - 128
    r = iota((256, 1), 0)
    wx = row * 8 - 128 + r // 32
    wy = xh * 32 - 128 + r % 32
    rad2 = wx * wx + wy * wy
    shells[...] = shell_sums(u * u + v * v, rad2)
    first[me1] = shells[...]

    @pl.loop(1, 32)
    def _(i):
        copy5(i).start()

    az = PHASE_RATE * (wz * wz).astype(F32)
    ar = PHASE_RATE * rad2.astype(F32)
    cz, sz = jnp.cos(az), jnp.sin(az)
    cr, sr = jnp.cos(ar), jnp.sin(ar)
    cos = (cr * cz - sr * sz).reshape(8, 32, 256)
    sin = (sr * cz + cr * sz).reshape(8, 32, 256)
    u, v = out[0], out[1]
    out[0] = u * cos + v * sin
    out[1] = v * cos - u * sin

    @pl.loop(1, 32)
    def _(i):
        copy5(i).wait_recv()

    mid[...] = jnp.sum(first[...], axis=0)
    second[yc] = mid[...]

    @pl.loop(1, 8)
    def _(j):
        copy6(j).start()

    @pl.loop(1, 8)
    def _(j):
        copy6(j).wait_recv()

    spectrum[...] = jnp.sum(second[...], axis=0) / counts[...]

    @pl.loop(0, 2)
    def _(h):
        @pl.loop(0, 4)
        def _(k):
            @pl.when(k > 0)
            def _():
                copy1(h, k, 0).wait_send()
                copy4(h, k, 0).wait_send()

            @pl.loop(1, 8)
            def _(i):
                copy1(h, k, i).wait_send()
                copy2(h, k, i).wait_send()
                copy3(h, k, i).wait_send()
                copy4(h, k, i).wait_send()

    @pl.loop(1, 32)
    def _(i):
        copy5(i).wait_send()

    @pl.loop(1, 8)
    def _(j):
        copy6(j).wait_send()


def tables():
    waves = np.arange(K, dtype=np.int64) - K // 2
    phase = (waves[:, None] * np.arange(N, dtype=np.int64)[None, :]) % N
    angle = phase.astype(np.float32) * np.float32(2.0 * math.pi / N)
    cos = np.cos(angle).astype(jnp.bfloat16)
    sin = np.sin(angle).astype(jnp.bfloat16)
    fwd = np.concatenate([cos, sin], axis=0)
    inv = np.concatenate([cos.T, sin.T], axis=1)
    h, g, c, s, z = np.meshgrid(*(np.arange(n) for n in (2, 4, 2, 8, 8)), indexing="ij")
    point = ((g * 8 + s) * 16 + h * 8 + z).reshape(-1)
    is_re = (c.reshape(-1) == 0)[:, None]
    ct, st = cos.T[point], sin.T[point]
    last = np.concatenate([np.where(is_re, ct, st), np.where(is_re, -st, ct)], axis=1)
    sq = waves * waves
    q = (sq[:, None] + sq[None, :]).reshape(-1)
    pairs = np.bincount(q, minlength=2 * (K // 2) ** 2 + 1)
    counts = np.zeros(K, np.float64)
    radii = np.nonzero(pairs)[0]
    for w2 in sq:
        shell = np.floor(np.sqrt((radii + w2).astype(np.float64)) + 0.5).astype(np.int64)
        counts += np.bincount(shell, weights=pairs[radii], minlength=K)[:K]
    return fwd, np.ascontiguousarray(inv), last, np.maximum(counts, 1.0).astype(np.float32).reshape(1, K)


VMEM = pl.BlockSpec(memory_space=pltpu.VMEM)
HBM = pl.BlockSpec(memory_space=pltpu.HBM)


def body(spectral_field, fwd, inv, last, counts):
    updated, spectrum = pl.pallas_call(
        transform_kernel,
        out_shape=(
            jax.ShapeDtypeStruct((2, 8, 32, 256), F32),
            jax.ShapeDtypeStruct((1, 256), F32),
        ),
        in_specs=[HBM, HBM, HBM, HBM, VMEM],
        out_specs=(VMEM, VMEM),
        scratch_shapes=[
            pltpu.VMEM((2, 8, 32, 256), F32),
            pltpu.VMEM((512, 512), BF16),
            pltpu.VMEM((512, 512), BF16),
            pltpu.VMEM((1024, 512), BF16),
            pltpu.VMEM((512, 512), BF16),
            pltpu.VMEM((128, 128), BF16),
            pltpu.VMEM((1024, 1024), BF16),
            pltpu.VMEM((2, 4, 8, 2, 8, 256), BF16),
            pltpu.VMEM((2, 4, 8, 2, 8, 256), BF16),
            pltpu.VMEM((2, 8, 8, 256), BF16),
            pltpu.VMEM((2, 8, 4, 4, 2, 8, 128), BF16),
            pltpu.VMEM((2, 4, 8, 4, 2, 8, 128), BF16),
            pltpu.VMEM((2, 512, 256), BF16),
            pltpu.VMEM((2, 8, 4, 4, 2, 8, 128), BF16),
            pltpu.VMEM((2, 8, 4, 4, 2, 8, 128), BF16),
            pltpu.VMEM((2, 4, 8, 32, 128), BF16),
            pltpu.VMEM((2, 4, 8, 32, 128), BF16),
            pltpu.VMEM((8, 32, 1024), BF16),
            pltpu.VMEM((1, 256), F32),
            pltpu.VMEM((32, 1, 256), F32),
            pltpu.VMEM((8, 1, 256), F32),
            pltpu.VMEM((1, 256), F32),
        ] + [pltpu.SemaphoreType.DMA((2, 4, 8))] * 8 + [
            pltpu.SemaphoreType.DMA((4,)),
            pltpu.SemaphoreType.DMA((32,)),
            pltpu.SemaphoreType.DMA((32,)),
            pltpu.SemaphoreType.DMA((8,)),
            pltpu.SemaphoreType.DMA((8,)),
        ],
        compiler_params=pltpu.CompilerParams(
            collective_id=0, has_side_effects=True, vmem_limit_bytes=67000000),
        name="transforms",
    )(spectral_field, fwd, inv, last, counts)
    return updated, spectrum.reshape(256)


def solution(mesh):
    consts = tables()
    step = functools.partial(jax.shard_map, mesh=mesh, check_vma=False)

    def run(spectral_field):
        return step(
            lambda f: body(f, *(jnp.asarray(c) for c in consts)),
            in_specs=(P(None, "row", "col", None),),
            out_specs=(P(None, "row", "col", None), P()),
        )(spectral_field)

    return run
```

time: 83.4 us -> 73.6 us (0.88)
  Pallas kernels: 80.2 us -> 70.4 us
    pallas_call x1, Pallas kernels: 80.2 us -> 70.4 us  [body(): pl.pallas_call(transform_kernel, out_shape=(jax.ShapeDtypeStruct((2, 8, 3...]
where the time goes in v2:
time: 73.6 us; the launch traced here: 73.5 us
  Pallas kernels  70.4 us (96%)
  local copies, waits for them, and re-layouts  2.45 us (3%)
    pallas_call x1, Pallas kernels, body(): pl.pallas_call(transform_kernel, out_shape=(jax.ShapeDtypeStruct((2, 8, 3...  70.4 us
    unnamed x4, local copies, waits for them, and re-layouts  2.45 us

profile of v2, /device:TPU:1, one launch (start us, length us, event | category | flops | bytes accessed | tf_op | source)
XLA Modules:
  0.0 73.5 jit_solution(11426256319136187598)
XLA Ops:
  0.6 70.4 %transforms.1 = (f32[2,8,32,256]{3,2,1,0:T(8,128)}, f32[1,256]{1,0:T(1,128)}) custom-call(f32[2,8,32,256]{3,2,1,0:T(8,128)} %field_hbm.1, bf16[512,512]{1,0:T(8,128)(2,1)} %constant.8.clone.fwd_hbm, bf16[512,512]{1,0:T(8,128)(2,1)} %constant.9.clone.inv_hbm, bf16[1024,512]{1,0:T(8,128)(2,1)} %constant.10.clone.last_hbm, f32[1,256]{1,0:T(1,128)} %constant.11.clone.counts), custom_call_target="tpu_custom_call" | custom-call | tf_op jit(solution)/shard_map/transforms/pallas_call | solution.py:419
  71.0 0.0 copy-start
  71.0 1.9 %copy.9 = f32[2,8,32,256]{3,2,1,0:T(8,128)} copy(f32[2,8,32,256]{3,2,1,0:T(8,128)} %get-tuple-element.8) | data formatting | bytes 1048576
  72.9 0.0 copy-done
  72.9 0.6 copy.10
Async XLA Ops:
  71.0 1.9 %copy-start = (f32[1,256]{1,0:T(1,128)S(1)}, f32[1,256]{1,0:T(1,128)}, u32[]{:S(2)}) copy-start(f32[1,256]{1,0:T(1,128)} %get-tuple-element.5) | copy-start | bytes 3076

commit v3 on v2

--- a/solution.py
+++ b/solution.py
@@ -33,17 +33,25 @@
     return jnp.where(hit, 1.0, 0.0).astype(BF16)
 
 
-def shell_sums(energy, r2):
+def shell_room(rad2, part):
+    s = iota((1, 128), 1) + part * 128
+    return s * s + s - rad2
+
+
+def shell_reach(rad2, part):
+    room = jnp.maximum(shell_room(rad2, part), 0).astype(F32)
+    return jnp.minimum(jnp.sqrt(room + 0.5).astype(jnp.int32), 127)
+
+
+def shell_sums(energy, rad2, reach):
     j = jnp.abs(iota((256, 128), 0) - 128)
     within = jnp.where(j <= iota((256, 128), 1), 1.0, 0.0)
     prefix = lax.dot_general(energy, within, (((1,), (0,)), ((), ())),
                              preferred_element_type=F32, precision=lax.Precision.HIGHEST)
     parts = []
-    for t in range(2):
-        s = iota((1, 128), 1) + t * 128
-        room = s * s + s - r2
-        m = jnp.sqrt(jnp.maximum(room, 0).astype(F32) + 0.5).astype(jnp.int32)
-        inner = jnp.take_along_axis(prefix, jnp.minimum(m, 127), axis=1, mode="promise_in_bounds")
+    for part in range(2):
+        room = shell_room(rad2, part)
+        inner = jnp.take_along_axis(prefix, reach[part], axis=1, mode="promise_in_bounds")
         total = jnp.where(room >= 0, inner, 0.0) + jnp.where(room >= 128 * 128, energy[:, :1], 0.0)
         parts.append(jnp.sum(total, axis=0, keepdims=True))
     lane = iota((1, 256), 1)
@@ -53,8 +61,8 @@
 
 
 def transform_kernel(
-    field_hbm, fwd_hbm, inv_hbm, last_hbm, counts, out, spectrum,
-    field, fwd, inv, last, p1, p2, p3, aout, bin_, yb, bout, cin, cub, cout, din, dout, ein, zb,
+    field_hbm, fwd_hbm, inv_hbm, last_hbm, counts_hbm, out, spectrum,
+    field, fwd, inv, last, counts, p1, p2, p3, aout, bin_, yb, bout, cin, cub, cout, din, dout, ein, zb, reach,
     shells, first, second, mid,
     s1, r1, s2, r2, s3, r3, s4, r4, load_sem, s5, r5, s6, r6,
 ):
@@ -74,6 +82,7 @@
         pltpu.make_async_copy(inv_hbm, inv, load_sem.at[1]),
         pltpu.make_async_copy(fwd_hbm, fwd, load_sem.at[2]),
         pltpu.make_async_copy(last_hbm, last, load_sem.at[3]),
+        pltpu.make_async_copy(counts_hbm, counts, load_sem.at[4]),
     ]
     for load in loads:
         load.start()
@@ -95,34 +104,55 @@
             device_id_type=pl.DeviceIdType.MESH,
         )
 
+    def wait(ref, sem):
+        pltpu.make_async_copy(ref, ref, sem).wait()
+
     def copy1(h, k, i):
-        zd = (zl + 4 - k) % 4
+        zd = (zl + 6 - k) % 4
         xd = (xh + i) % 8
-        return remote(aout.at[h, zd, xd], bin_.at[h, zl, xh], s1.at[h, k, i], r1.at[h, k, i], zd * 8 + yc, xd)
+        return remote(aout.at[h, zd, xd], bin_.at[h, zl, xh], s1.at[h, k], r1.at[h, k], zd * 8 + yc, xd)
 
     def copy2(h, k, j):
-        zs = (zl + k) % 4
+        zs = (zl + k + 2) % 4
         yd = (yc + j) % 8
-        return remote(bout.at[h, yd, zs], cin.at[h, zs, yc], s2.at[h, k, j], r2.at[h, k, j], zl * 8 + yd, xh)
+        return remote(bout.at[h, yd, zs], cin.at[h, zs, yc], s2.at[h, k], r2.at[h, k], zl * 8 + yd, xh)
 
     def copy3(h, k, j):
-        zs = (zl + k) % 4
+        zs = (zl + k + 3) % 4
         yd = (yc + j) % 8
-        return remote(cout.at[h, yd, zs], din.at[h, yc, zs], s3.at[h, k, j], r3.at[h, k, j], zl * 8 + yd, xh)
+        return remote(cout.at[h, yd, zs], din.at[h, yc, zs], s3.at[h, k], r3.at[h, k], zl * 8 + yd, xh)
 
     def copy4(h, k, i):
-        zd = (zl + k) % 4
+        zd = (zl + k + 3) % 4
         xd = (xh + i) % 8
-        return remote(dout.at[h, zd, xd], ein.at[h, zl, xh], s4.at[h, k, i], r4.at[h, k, i], zd * 8 + yc, xd)
+        return remote(dout.at[h, zd, xd], ein.at[h, zl, xh], s4.at[h, k], r4.at[h, k], zd * 8 + yc, xd)
+
+    def start_all(copy, h, k, own):
+        @pl.when(k != own)
+        def _():
+            copy(h, k, 0).start()
+
+        @pl.loop(1, 8)
+        def _(i):
+            copy(h, k, i).start()
+
+    def wait_all(ref, sem, h, k, own):
+        @pl.when(k != own)
+        def _():
+            wait(ref.at[h, 0], sem.at[h, k])
+
+        @pl.when(k == own)
+        def _():
+            wait(ref.at[h, 0, pl.ds(0, 7)], sem.at[h, k])
 
     me1 = zl * 8 + xh
 
     def copy5(i):
         d = (me1 + i) % 32
-        return remote(shells, first.at[me1], s5.at[i], r5.at[i], (d // 8) * 8 + yc, d % 8)
+        return remote(shells, first.at[me1], s5.at[0], r5.at[0], (d // 8) * 8 + yc, d % 8)
 
     def copy6(j):
-        return remote(mid, second.at[yc], s6.at[j], r6.at[j], zl * 8 + (yc + j) % 8, xh)
+        return remote(mid, second.at[yc], s6.at[0], r6.at[0], zl * 8 + (yc + j) % 8, xh)
 
     j1 = iota((128, 512), 1)
     f1 = ((j1 // 32) % 4) * 128 + (j1 // 128) * 32 + j1 % 32
@@ -167,21 +197,24 @@
 
     @pl.loop(0, 2)
     def _(h):
-        @pl.loop(1, 8)
-        def _(i):
-            copy1(h, 0, i).start()
-
-        @pl.loop(1, 4)
-        def _(k):
-            @pl.loop(0, 8)
-            def _(i):
-                copy1(h, k, i).start()
+        @pl.loop(0, 4)
+        def _(k):
+            start_all(copy1, h, k, 2)
+
+    wz = iota((1, 256), 1) - 128
+    r = iota((256, 1), 0)
+    wx = row * 8 - 128 + r // 32
+    wy = xh * 32 - 128 + r % 32
+    rad2 = wx * wx + wy * wy
+    for part in range(2):
+        reach[part] = shell_reach(rad2, part)
 
     loads[2].wait()
     loads[3].wait()
+    loads[4].wait()
 
     def stage_b(h, k):
-        zs = (zl + k) % 4
+        zs = (zl + k + 2) % 4
         parts = []
         for ht in range(2):
             for xt in range(2):
@@ -211,14 +244,7 @@
     def _(h):
         @pl.loop(0, 4)
         def _(k):
-            @pl.when(k > 0)
-            def _():
-                copy1(h, k, 0).wait_recv()
-
-            @pl.loop(1, 8)
-            def _(i):
-                copy1(h, k, i).wait_recv()
-
+            wait_all(bin_, r1, h, k, 2)
             stage_b(h, k)
 
             @pl.loop(1, 8)
@@ -251,9 +277,7 @@
     def _(h):
         @pl.loop(0, 4)
         def _(k):
-            @pl.loop(1, 8)
-            def _(j):
-                copy2(h, k, j).wait_recv()
+            wait(cin.at[h, 0, pl.ds(0, 7)], r2.at[h, k])
 
         @pl.loop(0, 2)
         def _(z):
@@ -271,7 +295,7 @@
         din[h, yc] = cout[h, yc]
 
     def stage_d(h, k):
-        zs = (zl + k) % 4
+        zs = (zl + k + 3) % 4
         r = []
         for c in range(2):
             r.append(jnp.concatenate([
@@ -284,51 +308,30 @@
     def _(h):
         @pl.loop(0, 4)
         def _(k):
-            @pl.loop(1, 8)
-            def _(j):
-                copy3(h, k, j).wait_recv()
-
+            wait(din.at[h, pl.ds(0, 7), 0], r3.at[h, k])
             stage_d(h, k)
-
-            @pl.when(k > 0)
-            def _():
-                copy4(h, k, 0).start()
-
-            @pl.loop(1, 8)
-            def _(i):
-                copy4(h, k, i).start()
+            start_all(copy4, h, k, 1)
 
         ein[h, zl, xh] = dout[h, zl, xh]
 
     for h in range(2):
         @pl.loop(0, 4)
         def _(k, h=h):
-            @pl.when(k > 0)
-            def _():
-                copy4(h, k, 0).wait_recv()
-
-            @pl.loop(1, 8)
-            def _(i):
-                copy4(h, k, i).wait_recv()
+            wait_all(ein, r4, h, k, 1)
 
         parts = [jnp.concatenate([ein[h, g, s] for s in range(8)], axis=1) for g in range(4)]
         o = mm(jnp.concatenate(parts, axis=0), p3[...]).astype(BF16)
         for g in range(4):
             for x in range(8):
-                zb[x, :, (h * 4 + g) * 128:(h * 4 + g) * 128 + 128] = o[g * 32:g * 32 + 32, x * 128:x * 128 + 128]
-    nl = mm(zb[...].reshape(256, 1024), last[...]) * (1.0 / 32.0)
-    nl_re, nl_im = nl[:, :256], nl[:, 256:]
-    u = field[0].reshape(256, 256) - nl_im
-    v = field[1].reshape(256, 256) + nl_re
-    out[0] = u.reshape(8, 32, 256)
-    out[1] = v.reshape(8, 32, 256)
-
-    wz = iota((1, 256), 1) - 128
-    r = iota((256, 1), 0)
-    wx = row * 8 - 128 + r // 32
-    wy = xh * 32 - 128 + r % 32
-    rad2 = wx * wx + wy * wy
-    shells[...] = shell_sums(u * u + v * v, rad2)
+                zb[h, x, :, g * 128:g * 128 + 128] = o[g * 32:g * 32 + 32, x * 128:x * 128 + 128]
+        nl = mm(zb[h].reshape(256, 512), last[h * 512:h * 512 + 512, :]) * (1.0 / 32.0)
+        base = field if h == 0 else out
+        u = base[0].reshape(256, 256) - nl[:, 256:]
+        v = base[1].reshape(256, 256) + nl[:, :256]
+        out[0] = u.reshape(8, 32, 256)
+        out[1] = v.reshape(8, 32, 256)
+
+    shells[...] = shell_sums(u * u + v * v, rad2, reach)
     first[me1] = shells[...]
 
     @pl.loop(1, 32)
@@ -345,9 +348,7 @@
     out[0] = u * cos + v * sin
     out[1] = v * cos - u * sin
 
-    @pl.loop(1, 32)
-    def _(i):
-        copy5(i).wait_recv()
+    wait(first.at[pl.ds(0, 31)], r5.at[0])
 
     mid[...] = jnp.sum(first[...], axis=0)
     second[yc] = mid[...]
@@ -356,9 +357,7 @@
     def _(j):
         copy6(j).start()
 
-    @pl.loop(1, 8)
-    def _(j):
-        copy6(j).wait_recv()
+    wait(second.at[pl.ds(0, 7)], r6.at[0])
 
     spectrum[...] = jnp.sum(second[...], axis=0) / counts[...]
 
@@ -366,25 +365,13 @@
     def _(h):
         @pl.loop(0, 4)
         def _(k):
-            @pl.when(k > 0)
-            def _():
-                copy1(h, k, 0).wait_send()
-                copy4(h, k, 0).wait_send()
-
-            @pl.loop(1, 8)
-            def _(i):
-                copy1(h, k, i).wait_send()
-                copy2(h, k, i).wait_send()
-                copy3(h, k, i).wait_send()
-                copy4(h, k, i).wait_send()
-
-    @pl.loop(1, 32)
-    def _(i):
-        copy5(i).wait_send()
-
-    @pl.loop(1, 8)
-    def _(j):
-        copy6(j).wait_send()
+            wait_all(aout, s1, h, k, 2)
+            wait(bout.at[h, pl.ds(0, 7), 0], s2.at[h, k])
+            wait(cout.at[h, pl.ds(0, 7), 0], s3.at[h, k])
+            wait_all(dout, s4, h, k, 1)
+
+    wait(first.at[pl.ds(0, 31)], s5.at[0])
+    wait(second.at[pl.ds(0, 7)], s6.at[0])
 
 
 def tables():
@@ -419,16 +406,17 @@
     updated, spectrum = pl.pallas_call(
         transform_kernel,
         out_shape=(
-            jax.ShapeDtypeStruct((2, 8, 32, 256), F32),
-            jax.ShapeDtypeStruct((1, 256), F32),
+            pltpu.VMEM((2, 8, 32, 256), F32),
+            pltpu.VMEM((1, 256), F32),
         ),
-        in_specs=[HBM, HBM, HBM, HBM, VMEM],
+        in_specs=[HBM] * 5,
         out_specs=(VMEM, VMEM),
         scratch_shapes=[
             pltpu.VMEM((2, 8, 32, 256), F32),
             pltpu.VMEM((512, 512), BF16),
             pltpu.VMEM((512, 512), BF16),
             pltpu.VMEM((1024, 512), BF16),
+            pltpu.VMEM((1, 256), F32),
             pltpu.VMEM((512, 512), BF16),
             pltpu.VMEM((128, 128), BF16),
             pltpu.VMEM((1024, 1024), BF16),
@@ -442,22 +430,18 @@
             pltpu.VMEM((2, 8, 4, 4, 2, 8, 128), BF16),
             pltpu.VMEM((2, 4, 8, 32, 128), BF16),
             pltpu.VMEM((2, 4, 8, 32, 128), BF16),
-            pltpu.VMEM((8, 32, 1024), BF16),
+            pltpu.VMEM((2, 8, 32, 512), BF16),
+            pltpu.VMEM((2, 256, 128), jnp.int32),
             pltpu.VMEM((1, 256), F32),
             pltpu.VMEM((32, 1, 256), F32),
             pltpu.VMEM((8, 1, 256), F32),
             pltpu.VMEM((1, 256), F32),
-        ] + [pltpu.SemaphoreType.DMA((2, 4, 8))] * 8 + [
-            pltpu.SemaphoreType.DMA((4,)),
-            pltpu.SemaphoreType.DMA((32,)),
-            pltpu.SemaphoreType.DMA((32,)),
-            pltpu.SemaphoreType.DMA((8,)),
-            pltpu.SemaphoreType.DMA((8,)),
-        ],
+        ] + [pltpu.SemaphoreType.DMA((2, 4))] * 8 + [pltpu.SemaphoreType.DMA((5,))] + [
+            pltpu.SemaphoreType.DMA((1,))] * 4,
         compiler_params=pltpu.CompilerParams(
-            collective_id=0, has_side_effects=True, vmem_limit_bytes=67000000),
+            collective_id=0, has_side_effects=True, vmem_limit_bytes=50 * 1024 * 1024),
         name="transforms",
-    )(spectral_field, fwd, inv, last, counts)
+    )(*(pltpu.with_memory_space_constraint(x, pltpu.HBM) for x in (spectral_field, fwd, inv, last, counts)))
     return updated, spectrum.reshape(256)
 
 

time: 73.6 us -> 65.6 us (0.89)
  Pallas kernels: 70.4 us -> 63.5 us
  local copies, waits for them, and re-layouts: 2.45 us -> 1.36 us
    pallas_call x1, Pallas kernels: 70.4 us -> 63.5 us  [body(): pl.pallas_call(transform_kernel, out_shape=(pltpu.VMEM((2, 8, 32, 256), F...]
    unnamed x4 -> x2, local copies, waits for them, and re-layouts: 2.45 us -> 1.36 us
where the time goes in v3:
time: 65.6 us; the launch traced here: 65.5 us
  Pallas kernels  63.5 us (97%)
  local copies, waits for them, and re-layouts  1.36 us (2%)
    pallas_call x1, Pallas kernels, body(): pl.pallas_call(transform_kernel, out_shape=(pltpu.VMEM((2, 8, 32, 256), F...  63.5 us
    unnamed x2, local copies, waits for them, and re-layouts  1.36 us

profile of v3, /device:TPU:1, one launch (start us, length us, event | category | flops | bytes accessed | tf_op | source)
XLA Modules:
  0.0 65.5 jit_solution(6948981481081663973)
XLA Ops:
  0.6 63.5 %transforms.1 = (f32[2,8,32,256]{3,2,1,0:T(8,128)S(1)}, f32[1,256]{1,0:T(1,128)S(1)}) custom-call(f32[2,8,32,256]{3,2,1,0:T(8,128)} %field_hbm.1, bf16[512,512]{1,0:T(8,128)(2,1)} %constant.8.clone.fwd_hbm, bf16[512,512]{1,0:T(8,128)(2,1)} %constant.9.clone.inv_hbm, bf16[1024,512]{1,0:T(8,128)(2,1)} %constant.10.clone.last_hbm, ...), custom_call_target="tpu_custom_call" | custom-call | tf_op jit(solution)/shard_map/transforms/pallas_call | solution.py:406
  64.1 0.8 %copy.9 = f32[2,8,32,256]{3,2,1,0:T(8,128)} copy(f32[2,8,32,256]{3,2,1,0:T(8,128)S(1)} %get-tuple-element.6) | data formatting | bytes 1048576
  64.9 0.6 copy.10

commit v4 on v3

--- a/solution.py
+++ b/solution.py
@@ -62,7 +62,7 @@
 
 def transform_kernel(
     field_hbm, fwd_hbm, inv_hbm, last_hbm, counts_hbm, out, spectrum,
-    field, fwd, inv, last, counts, p1, p2, p3, aout, bin_, yb, bout, cin, cub, cout, din, dout, ein, zb, reach,
+    field, fwd, inv, last, counts, p1, p2, p3, eye, aout, bin_, xr, bout, cin, yb, cub, xb, cout, din, dout, ein, zb, reach,
     shells, first, second, mid,
     s1, r1, s2, r2, s3, r3, s4, r4, load_sem, s5, r5, s6, r6,
 ):
@@ -120,7 +120,7 @@
     def copy3(h, k, j):
         zs = (zl + k + 3) % 4
         yd = (yc + j) % 8
-        return remote(cout.at[h, yd, zs], din.at[h, yc, zs], s3.at[h, k], r3.at[h, k], zl * 8 + yd, xh)
+        return remote(cout.at[h, yd, zs], din.at[h, zs, yc], s3.at[h, k], r3.at[h, k], zl * 8 + yd, xh)
 
     def copy4(h, k, i):
         zd = (zl + k + 3) % 4
@@ -165,8 +165,9 @@
     q2 = iota((128, 128), 0)
     p2[...] = one_hot(iota((128, 128), 1) == (q2 // 64) * 64 + (q2 % 8) * 8 + (q2 // 8) % 8)
 
+    eye[...] = one_hot(iota((256, 256), 0) == iota((256, 256), 1))
     j3 = iota((128, 1024), 1)
-    f3 = ((j3 // 8) % 8) * 128 + ((j3 // 64) % 2) * 64 + (j3 % 8) * 8 + j3 // 128
+    f3 = ((j3 // 8) % 8) * 128 + (j3 % 8) * 16 + ((j3 // 64) % 2) * 8 + j3 // 128
 
     @pl.loop(0, 8)
     def _(b):
@@ -227,17 +228,11 @@
                 base = (ht * 2 + xt) * 16
                 for c in range(2):
                     for x in range(4):
-                        yb[c, xt * 4 + x, :, ht * 128:ht * 128 + 128] = (
+                        xr[c, xt * 4 + x, :, ht * 128:ht * 128 + 128] = (
                             o[base + c * 8:base + c * 8 + 8, x * 128:x * 128 + 128].astype(BF16))
-        q = mm(p2[...], yb[...].reshape(128, 256)).astype(BF16)
-        mc = mm(q, fwd[:256, :])
-        ms = mm(q, fwd[256:, :])
-        pair = ((mc[:64] - ms[64:]) * (1.0 / 16.0), (ms[:64] + mc[64:]) * (1.0 / 16.0))
+        q = mm(p2[...], xr[...].reshape(128, 256)).reshape(2, 8, 8, 256)
         for c in range(2):
-            for y in range(4):
-                w = pair[c][:, y * 128:y * 128 + 128].reshape(2, 4, 8, 128)
-                for zh in range(2):
-                    bout[h, y * 2 + zh, zs, :, c] = w[zh].astype(BF16)
+            bout[h, :, zs, c] = q[c].astype(BF16)
         cin[h, zs, yc] = bout[h, yc, zs]
 
     @pl.loop(0, 2)
@@ -251,8 +246,19 @@
             def _(j):
                 copy2(h, k, j).start()
 
-    def stage_c(h, z, slot):
-        d = jnp.concatenate([cin[h, :, :, z, 0].reshape(256, 128), cin[h, :, :, z, 1].reshape(256, 128)], axis=1)
+    def plane_y(h):
+        for half in range(2):
+            d = jnp.concatenate(
+                [cin[h, half * 2:half * 2 + 2, :, c].reshape(128, 256) for c in range(2)], axis=0)
+            mc = mm(d, fwd[:256, :])
+            ms = mm(d, fwd[256:, :])
+            pair = ((mc[:128] - ms[128:]) * (1.0 / 16.0), (ms[:128] + mc[128:]) * (1.0 / 16.0))
+            for c in range(2):
+                for y in range(4):
+                    yb[y, c, half * 128:half * 128 + 128, :] = pair[c][:, y * 128:y * 128 + 128].astype(BF16)
+
+    def plane_x(y, slot):
+        d = jnp.concatenate([yb[y, 0], yb[y, 1]], axis=1)
         d = jnp.concatenate([d, jnp.concatenate([-d[:, 128:], d[:, :128]], axis=1)], axis=0)
         for half in range(2):
             rows = slice(half * 256, half * 256 + 256)
@@ -262,16 +268,25 @@
             cub[slot, rows, :128] = (gain * re).astype(BF16)
             cub[slot, rows, 128:] = (gain * im).astype(BF16)
 
-    def stage_c_back(h, z, slot):
+    def plane_x_back(y, slot):
         m = mm(fwd[...], cub[slot])
-        pair = (
-            (m[:256, :128] + m[256:, 128:]) * (1.0 / 32.0),
-            (m[:256, 128:] - m[256:, :128]) * (1.0 / 32.0),
-        )
-        for c in range(2):
-            v = pair[c].reshape(4, 8, 8, 128)
-            for q in range(4):
-                cout[h, :, q, z, c] = v[q].astype(BF16)
+        xb[y, 0] = ((m[:256, :128] + m[256:, 128:]) * (1.0 / 32.0)).astype(BF16)
+        xb[y, 1] = ((m[:256, 128:] - m[256:, :128]) * (1.0 / 32.0)).astype(BF16)
+
+    def plane_y_back(h):
+        for half in range(2):
+            rows = slice(half * 128, half * 128 + 128)
+            d = jnp.concatenate(
+                [jnp.concatenate([xb[y, c, rows, :] for y in range(4)], axis=1) for c in range(2)], axis=0)
+            m = mm(d, inv[...])
+            pair = (
+                (m[:128, :256] + m[128:, 256:]) * (1.0 / 32.0),
+                (m[128:, :256] - m[:128, 256:]) * (1.0 / 32.0),
+            )
+            for c in range(2):
+                v = pair[c].reshape(2, 8, 8, 256)
+                for q in range(2):
+                    cout[h, :, half * 2 + q, c] = v[q].astype(BF16)
 
     @pl.loop(0, 2)
     def _(h):
@@ -279,12 +294,16 @@
         def _(k):
             wait(cin.at[h, 0, pl.ds(0, 7)], r2.at[h, k])
 
+        plane_y(h)
+
         @pl.loop(0, 2)
-        def _(z):
-            stage_c(h, 2 * z, 0)
-            stage_c(h, 2 * z + 1, 1)
-            stage_c_back(h, 2 * z, 0)
-            stage_c_back(h, 2 * z + 1, 1)
+        def _(y):
+            plane_x(2 * y, 0)
+            plane_x(2 * y + 1, 1)
+            plane_x_back(2 * y, 0)
+            plane_x_back(2 * y + 1, 1)
+
+        plane_y_back(h)
 
         @pl.loop(0, 4)
         def _(k):
@@ -292,23 +311,18 @@
             def _(j):
                 copy3(h, k, j).start()
 
-        din[h, yc] = cout[h, yc]
+        din[h, :, yc] = cout[h, yc]
 
     def stage_d(h, k):
         zs = (zl + k + 3) % 4
-        r = []
-        for c in range(2):
-            r.append(jnp.concatenate([
-                jnp.concatenate([din[h, y * 2 + zh, zs, :, c].reshape(32, 128) for zh in range(2)], axis=0)
-                for y in range(4)], axis=1))
-        o = mmt(fwd[:256, :], jnp.concatenate(r, axis=0)) + mmt(fwd[256:, :], jnp.concatenate([r[1], -r[0]], axis=0))
-        dout[h, zs] = (o * (1.0 / 32.0)).astype(BF16).reshape(8, 32, 128)
+        o = mmt(eye[...], din[h, zs].reshape(128, 256))
+        dout[h, zs] = o.astype(BF16).reshape(8, 32, 128)
 
     @pl.loop(0, 2)
     def _(h):
         @pl.loop(0, 4)
         def _(k):
-            wait(din.at[h, pl.ds(0, 7), 0], r3.at[h, k])
+            wait(din.at[h, 0, pl.ds(0, 7)], r3.at[h, k])
             stage_d(h, k)
             start_all(copy4, h, k, 1)
 
@@ -420,14 +434,17 @@
             pltpu.VMEM((512, 512), BF16),
             pltpu.VMEM((128, 128), BF16),
             pltpu.VMEM((1024, 1024), BF16),
+            pltpu.VMEM((256, 256), BF16),
             pltpu.VMEM((2, 4, 8, 2, 8, 256), BF16),
             pltpu.VMEM((2, 4, 8, 2, 8, 256), BF16),
             pltpu.VMEM((2, 8, 8, 256), BF16),
-            pltpu.VMEM((2, 8, 4, 4, 2, 8, 128), BF16),
-            pltpu.VMEM((2, 4, 8, 4, 2, 8, 128), BF16),
+            pltpu.VMEM((2, 8, 4, 2, 8, 256), BF16),
+            pltpu.VMEM((2, 4, 8, 2, 8, 256), BF16),
+            pltpu.VMEM((4, 2, 256, 128), BF16),
             pltpu.VMEM((2, 512, 256), BF16),
-            pltpu.VMEM((2, 8, 4, 4, 2, 8, 128), BF16),
-            pltpu.VMEM((2, 8, 4, 4, 2, 8, 128), BF16),
+            pltpu.VMEM((4, 2, 256, 128), BF16),
+            pltpu.VMEM((2, 8, 4, 2, 8, 256), BF16),
+            pltpu.VMEM((2, 4, 8, 2, 8, 256), BF16),
             pltpu.VMEM((2, 4, 8, 32, 128), BF16),
             pltpu.VMEM((2, 4, 8, 32, 128), BF16),
             pltpu.VMEM((2, 8, 32, 512), BF16),

time: 65.6 us -> 63.6 us (0.970)
  Pallas kernels: 63.5 us -> 61.5 us
    pallas_call x1, Pallas kernels: 63.5 us -> 61.5 us  [body(): pl.pallas_call(transform_kernel, out_shape=(pltpu.VMEM((2, 8, 32, 256), F...]
where the time goes in v4:
time: 63.6 us; the launch traced here: 63.5 us
  Pallas kernels  61.5 us (97%)
  local copies, waits for them, and re-layouts  1.36 us (2%)
  between operations  0.64 us (1%)
    pallas_call x1, Pallas kernels, body(): pl.pallas_call(transform_kernel, out_shape=(pltpu.VMEM((2, 8, 32, 256), F...  61.5 us
    unnamed x2, local copies, waits for them, and re-layouts  1.36 us

profile of v4, /device:TPU:1, one launch (start us, length us, event | category | flops | bytes accessed | tf_op | source)
XLA Modules:
  0.0 63.5 jit_solution(3599275836584567630)
XLA Ops:
  0.6 61.5 %transforms.1 = (f32[2,8,32,256]{3,2,1,0:T(8,128)S(1)}, f32[1,256]{1,0:T(1,128)S(1)}) custom-call(f32[2,8,32,256]{3,2,1,0:T(8,128)} %field_hbm.1, bf16[512,512]{1,0:T(8,128)(2,1)} %constant.8.clone.fwd_hbm, bf16[512,512]{1,0:T(8,128)(2,1)} %constant.9.clone.inv_hbm, bf16[1024,512]{1,0:T(8,128)(2,1)} %constant.10.clone.last_hbm, ...), custom_call_target="tpu_custom_call" | custom-call | tf_op jit(solution)/shard_map/transforms/pallas_call | solution.py:420
  62.2 0.8 %copy.9 = f32[2,8,32,256]{3,2,1,0:T(8,128)} copy(f32[2,8,32,256]{3,2,1,0:T(8,128)S(1)} %get-tuple-element.6) | data formatting | bytes 1048576
  63.0 0.6 copy.10

commit v5 on v4

--- a/solution.py
+++ b/solution.py
@@ -84,7 +84,7 @@
         pltpu.make_async_copy(last_hbm, last, load_sem.at[3]),
         pltpu.make_async_copy(counts_hbm, counts, load_sem.at[4]),
     ]
-    for load in loads:
+    for load in loads[:2]:
         load.start()
 
     barrier = pltpu.get_barrier_semaphore()
@@ -128,7 +128,7 @@
         return remote(dout.at[h, zd, xd], ein.at[h, zl, xh], s4.at[h, k], r4.at[h, k], zd * 8 + yc, xd)
 
     def start_all(copy, h, k, own):
-        @pl.when(k != own)
+        @pl.when(jnp.asarray(k) != own)
         def _():
             copy(h, k, 0).start()
 
@@ -154,31 +154,13 @@
     def copy6(j):
         return remote(mid, second.at[yc], s6.at[0], r6.at[0], zl * 8 + (yc + j) % 8, xh)
 
-    j1 = iota((128, 512), 1)
-    f1 = ((j1 // 32) % 4) * 128 + (j1 // 128) * 32 + j1 % 32
-
-    @pl.loop(0, 4)
-    def _(b):
-        rows = pl.ds(pl.multiple_of(b * 128, 128), 128)
-        p1[rows, :] = one_hot(iota((128, 512), 0) + b * 128 == f1)
-
-    q2 = iota((128, 128), 0)
-    p2[...] = one_hot(iota((128, 128), 1) == (q2 // 64) * 64 + (q2 % 8) * 8 + (q2 // 8) % 8)
-
-    eye[...] = one_hot(iota((256, 256), 0) == iota((256, 256), 1))
-    j3 = iota((128, 1024), 1)
-    f3 = ((j3 // 8) % 8) * 128 + (j3 % 8) * 16 + ((j3 // 64) % 2) * 8 + j3 // 128
-
-    @pl.loop(0, 8)
-    def _(b):
-        rows = pl.ds(pl.multiple_of(b * 128, 128), 128)
-        p3[rows, :] = one_hot(iota((128, 1024), 0) + b * 128 == f3)
-
+    for load in loads[2:]:
+        load.start()
     loads[0].wait()
     loads[1].wait()
 
-    @pl.loop(0, 4)
-    def _(zd):
+    def stage_a(k):
+        zd = (zl + 6 - k) % 4
         rows = pl.ds(pl.multiple_of(zd * 128, 128), 128)
         c, s = inv[rows, :256], inv[rows, 256:]
         re = field[0].reshape(256, 256).astype(BF16)
@@ -192,15 +174,41 @@
             for h in range(2):
                 aout[h, zd, :, ri] = v[:, h].astype(BF16)
 
+    stage_a(0)
+    pl.semaphore_wait(barrier, 38)
+    start_all(copy1, 0, 0, 2)
+
+    @pl.loop(1, 4)
+    def _(k):
+        stage_a(k)
+        start_all(copy1, 0, k, 2)
+
+    @pl.loop(0, 4)
+    def _(k):
+        start_all(copy1, 1, k, 2)
+
     for h in range(2):
         bin_[h, zl, xh] = aout[h, zl, xh]
-    pl.semaphore_wait(barrier, 38)
-
-    @pl.loop(0, 2)
-    def _(h):
-        @pl.loop(0, 4)
-        def _(k):
-            start_all(copy1, h, k, 2)
+
+    j1 = iota((128, 512), 1)
+    f1 = ((j1 // 32) % 4) * 128 + (j1 // 128) * 32 + j1 % 32
+
+    @pl.loop(0, 4)
+    def _(b):
+        rows = pl.ds(pl.multiple_of(b * 128, 128), 128)
+        p1[rows, :] = one_hot(iota((128, 512), 0) + b * 128 == f1)
+
+    q2 = iota((128, 128), 0)
+    p2[...] = one_hot(iota((128, 128), 1) == (q2 // 64) * 64 + (q2 % 8) * 8 + (q2 // 8) % 8)
+
+    eye[...] = one_hot(iota((256, 256), 0) == iota((256, 256), 1))
+    j3 = iota((128, 1024), 1)
+    f3 = ((j3 // 8) % 8) * 128 + (j3 % 8) * 16 + ((j3 // 64) % 2) * 8 + j3 // 128
+
+    @pl.loop(0, 8)
+    def _(b):
+        rows = pl.ds(pl.multiple_of(b * 128, 128), 128)
+        p3[rows, :] = one_hot(iota((128, 1024), 0) + b * 128 == f3)
 
     wz = iota((1, 256), 1) - 128
     r = iota((256, 1), 0)

time: 63.6 us -> 63.4 us (level)
  no operation moved by 1% of the time
where the time goes in v5:
time: 63.4 us; the launch traced here: 63.3 us
  Pallas kernels  61.3 us (97%)
  local copies, waits for them, and re-layouts  1.36 us (2%)
  between operations  0.64 us (1%)
    pallas_call x1, Pallas kernels, body(): pl.pallas_call(transform_kernel, out_shape=(pltpu.VMEM((2, 8, 32, 256), F...  61.3 us
    unnamed x2, local copies, waits for them, and re-layouts  1.36 us

profile of v5, /device:TPU:1, one launch (start us, length us, event | category | flops | bytes accessed | tf_op | source)
XLA Modules:
  0.0 63.3 jit_solution(11482239348738285405)
XLA Ops:
  0.6 61.3 %transforms.1 = (f32[2,8,32,256]{3,2,1,0:T(8,128)S(1)}, f32[1,256]{1,0:T(1,128)S(1)}) custom-call(f32[2,8,32,256]{3,2,1,0:T(8,128)} %field_hbm.1, bf16[512,512]{1,0:T(8,128)(2,1)} %constant.8.clone.fwd_hbm, bf16[512,512]{1,0:T(8,128)(2,1)} %constant.9.clone.inv_hbm, bf16[1024,512]{1,0:T(8,128)(2,1)} %constant.10.clone.last_hbm, ...), custom_call_target="tpu_custom_call" | custom-call | tf_op jit(solution)/shard_map/transforms/pallas_call | solution.py:428
  61.9 0.8 %copy.9 = f32[2,8,32,256]{3,2,1,0:T(8,128)} copy(f32[2,8,32,256]{3,2,1,0:T(8,128)S(1)} %get-tuple-element.6) | data formatting | bytes 1048576
  62.7 0.6 copy.10

commit v6 on v5

--- a/solution.py
+++ b/solution.py
@@ -145,14 +145,18 @@
         def _():
             wait(ref.at[h, 0, pl.ds(0, 7)], sem.at[h, k])
 
-    me1 = zl * 8 + xh
+    xc, z_hi, yy, core = xh // 2, xh % 2, yc // 2, yc % 2
+    me1 = xc * 4 + yy
+    me2 = (z_hi * 4 + zl) * 2 + core
 
     def copy5(i):
-        d = (me1 + i) % 32
-        return remote(shells, first.at[me1], s5.at[0], r5.at[0], (d // 8) * 8 + yc, d % 8)
-
-    def copy6(j):
-        return remote(mid, second.at[yc], s6.at[0], r6.at[0], zl * 8 + (yc + j) % 8, xh)
+        d = (me1 + i) % 16
+        return remote(shells, first.at[me1], s5.at[0], r5.at[0], zl * 8 + (d % 4) * 2 + core, (d // 4) * 2 + z_hi)
+
+    def copy6(i):
+        d = (me2 + i) % 16
+        return remote(
+            mid, second.at[me2], s6.at[0], r6.at[0], ((d // 2) % 4) * 8 + yy * 2 + d % 2, xc * 2 + d // 8)
 
     for load in loads[2:]:
         load.start()
@@ -356,7 +360,7 @@
     shells[...] = shell_sums(u * u + v * v, rad2, reach)
     first[me1] = shells[...]
 
-    @pl.loop(1, 32)
+    @pl.loop(1, 16)
     def _(i):
         copy5(i).start()
 
@@ -370,16 +374,16 @@
     out[0] = u * cos + v * sin
     out[1] = v * cos - u * sin
 
-    wait(first.at[pl.ds(0, 31)], r5.at[0])
+    wait(first.at[pl.ds(0, 15)], r5.at[0])
 
     mid[...] = jnp.sum(first[...], axis=0)
-    second[yc] = mid[...]
-
-    @pl.loop(1, 8)
-    def _(j):
-        copy6(j).start()
-
-    wait(second.at[pl.ds(0, 7)], r6.at[0])
+    second[me2] = mid[...]
+
+    @pl.loop(1, 16)
+    def _(i):
+        copy6(i).start()
+
+    wait(second.at[pl.ds(0, 15)], r6.at[0])
 
     spectrum[...] = jnp.sum(second[...], axis=0) / counts[...]
 
@@ -392,8 +396,8 @@
             wait(cout.at[h, pl.ds(0, 7), 0], s3.at[h, k])
             wait_all(dout, s4, h, k, 1)
 
-    wait(first.at[pl.ds(0, 31)], s5.at[0])
-    wait(second.at[pl.ds(0, 7)], s6.at[0])
+    wait(first.at[pl.ds(0, 15)], s5.at[0])
+    wait(second.at[pl.ds(0, 15)], s6.at[0])
 
 
 def tables():
@@ -458,8 +462,8 @@
             pltpu.VMEM((2, 8, 32, 512), BF16),
             pltpu.VMEM((2, 256, 128), jnp.int32),
             pltpu.VMEM((1, 256), F32),
-            pltpu.VMEM((32, 1, 256), F32),
-            pltpu.VMEM((8, 1, 256), F32),
+            pltpu.VMEM((16, 1, 256), F32),
+            pltpu.VMEM((16, 1, 256), F32),
             pltpu.VMEM((1, 256), F32),
         ] + [pltpu.SemaphoreType.DMA((2, 4))] * 8 + [pltpu.SemaphoreType.DMA((5,))] + [
             pltpu.SemaphoreType.DMA((1,))] * 4,

time: 63.4 us -> 63.1 us (level)
  no operation moved by 1% of the time
where the time goes in v6:
time: 63.1 us; the launch traced here: 63 us
  Pallas kernels  61 us (97%)
  local copies, waits for them, and re-layouts  1.36 us (2%)
  between operations  0.64 us (1%)
    pallas_call x1, Pallas kernels, body(): pl.pallas_call(transform_kernel, out_shape=(pltpu.VMEM((2, 8, 32, 256), F...  61 us
    unnamed x2, local copies, waits for them, and re-layouts  1.36 us

profile of v6, /device:TPU:1, one launch (start us, length us, event | category | flops | bytes accessed | tf_op | source)
XLA Modules:
  0.0 63.0 jit_solution(9523785103839160609)
XLA Ops:
  0.6 61.0 %transforms.1 = (f32[2,8,32,256]{3,2,1,0:T(8,128)S(1)}, f32[1,256]{1,0:T(1,128)S(1)}) custom-call(f32[2,8,32,256]{3,2,1,0:T(8,128)} %field_hbm.1, bf16[512,512]{1,0:T(8,128)(2,1)} %constant.8.clone.fwd_hbm, bf16[512,512]{1,0:T(8,128)(2,1)} %constant.9.clone.inv_hbm, bf16[1024,512]{1,0:T(8,128)(2,1)} %constant.10.clone.last_hbm, ...), custom_call_target="tpu_custom_call" | custom-call | tf_op jit(solution)/shard_map/transforms/pallas_call | solution.py:432
  61.6 0.8 %copy.9 = f32[2,8,32,256]{3,2,1,0:T(8,128)} copy(f32[2,8,32,256]{3,2,1,0:T(8,128)S(1)} %get-tuple-element.6) | data formatting | bytes 1048576
  62.4 0.6 copy.10

commit v7 on v6

--- a/solution.py
+++ b/solution.py
@@ -308,8 +308,7 @@
 
         plane_y(h)
 
-        @pl.loop(0, 2)
-        def _(y):
+        for y in range(2):
             plane_x(2 * y, 0)
             plane_x(2 * y + 1, 1)
             plane_x_back(2 * y, 0)

time: 63.1 us -> 63.5 us (level)
  no operation moved by 1% of the time
where the time goes in v7:
time: 63.5 us; the launch traced here: 63.4 us
  Pallas kernels  61.4 us (97%)
  local copies, waits for them, and re-layouts  1.36 us (2%)
  between operations  0.64 us (1%)
    pallas_call x1, Pallas kernels, body(): pl.pallas_call(transform_kernel, out_shape=(pltpu.VMEM((2, 8, 32, 256), F...  61.4 us
    unnamed x2, local copies, waits for them, and re-layouts  1.36 us

profile of v7, /device:TPU:1, one launch (start us, length us, event | category | flops | bytes accessed | tf_op | source)
XLA Modules:
  0.0 63.4 jit_solution(9206786483912166760)
XLA Ops:
  0.6 61.4 %transforms.1 = (f32[2,8,32,256]{3,2,1,0:T(8,128)S(1)}, f32[1,256]{1,0:T(1,128)S(1)}) custom-call(f32[2,8,32,256]{3,2,1,0:T(8,128)} %field_hbm.1, bf16[512,512]{1,0:T(8,128)(2,1)} %constant.8.clone.fwd_hbm, bf16[512,512]{1,0:T(8,128)(2,1)} %constant.9.clone.inv_hbm, bf16[1024,512]{1,0:T(8,128)(2,1)} %constant.10.clone.last_hbm, ...), custom_call_target="tpu_custom_call" | custom-call | tf_op jit(solution)/shard_map/transforms/pallas_call | solution.py:431
  62.0 0.8 %copy.9 = f32[2,8,32,256]{3,2,1,0:T(8,128)} copy(f32[2,8,32,256]{3,2,1,0:T(8,128)S(1)} %get-tuple-element.6) | data formatting | bytes 1048576
  62.8 0.6 copy.10
